TPU v7x, 16 devices: a 4x2x1 block of a 4x4x8 slice. The times are simulated.
16 devices in a mesh: rep: 4 (over y, z, core), dp: 4 (over x).
Axes of the slice: x: 4, y: 2, z: 1, core: 2. Of those that a mesh axis runs over, the one named last changes fastest.
The devices are a block of a 4x4x8 slice.
Arguments:
- x: bfloat16 [16, 4096, 512], P(('rep', 'dp')), parts along dimension 0
- dy: bfloat16 [16, 4096, 512], P(('rep', 'dp')), parts along dimension 0
- w_gate: bfloat16 [2, 512, 1664], replicated
- w_up: bfloat16 [2, 512, 1664], replicated
- w_down: bfloat16 [2, 1664, 512], replicated
- m_w_gate: float32 [2, 512, 1664], replicated
- m_w_up: float32 [2, 512, 1664], replicated
- m_w_down: float32 [2, 1664, 512], replicated
- v_w_gate: float32 [2, 512, 1664], replicated
- v_w_up: float32 [2, 512, 1664], replicated
- v_w_down: float32 [2, 1664, 512], replicated
Outputs:
- output 1: bfloat16 [8, 512, 1664], P('rep'), parts along dimension 0
- output 2: bfloat16 [8, 512, 1664], P('rep'), parts along dimension 0
- output 3: bfloat16 [8, 1664, 512], P('rep'), parts along dimension 0
- output 4: float32 [8, 512, 1664], P('rep'), parts along dimension 0
- output 5: float32 [8, 512, 1664], P('rep'), parts along dimension 0
- output 6: float32 [8, 1664, 512], P('rep'), parts along dimension 0
- output 7: float32 [8, 512, 1664], P('rep'), parts along dimension 0
- output 8: float32 [8, 512, 1664], P('rep'), parts along dimension 0
- output 9: float32 [8, 1664, 512], P('rep'), parts along dimension 0
There are 4 independent parts. A program takes and returns all parts, laid end to end along the dimension named above; an argument that names none is the same for every part.
All inputs are finite; a program needn't handle non-finite values.
Results may differ from a plain program's by a relative error of at most 0.02.
Values are sent between devices in bfloat16 or wider.
A program may use at most 768 MiB of HBM per device.

v0:
```python
import jax
import jax.numpy as jnp
from jax import lax
from jax.sharding import PartitionSpec as P

NAMES = ("w_gate", "w_up", "w_down")


def matmul(a, w):
    return jnp.dot(a, w, preferred_element_type=jnp.float32).astype(jnp.bfloat16)


def normed(h):
    wide = h.astype(jnp.float32)
    scale = lax.rsqrt(jnp.mean(wide**2, -1, keepdims=True) + 1e-6)
    return (wide * scale).astype(jnp.bfloat16)


def layer(h, w):
    a = normed(h)
    gate = jnp.dot(a, w["w_gate"], preferred_element_type=jnp.float32)
    up = jnp.dot(a, w["w_up"], preferred_element_type=jnp.float32)
    return h + matmul((jax.nn.silu(gate) * up).astype(jnp.bfloat16), w["w_down"])


def adamw(w, m, v, g):
    m = 0.9 * m + 0.1 * g
    v = 0.95 * v + 0.05 * g * g
    step = m * lax.rsqrt(v + 1e-8) + 0.1 * w
    return (w - 0.02 * step).astype(jnp.bfloat16), m, v


def solution(mesh):
    def step(x, dy, *arrays):
        weights, m, v = (arrays[i : i + 3] for i in (0, 3, 6))
        layers = weights[0].shape[0]
        h, kept = x[0], []
        for number in range(layers):
            kept.append(h)
            h = layer(h, {name: w[number] for name, w in zip(NAMES, weights, strict=True)})
        by_h, summed = dy[0], [None] * layers
        for number in reversed(range(layers)):
            _, back = jax.vjp(lambda w, h: layer(h, w), {name: w[number] for name, w in zip(NAMES, weights, strict=True)}, kept[number])
            by_w, by_h = back(by_h)
            summed[number] = [lax.psum(by_w[name], "dp") for name in NAMES]
        gradients = [jnp.stack([summed[number][i] for number in range(layers)]).astype(jnp.float32) for i in range(3)]
        new = [adamw(w.astype(jnp.float32), m, v, g) for w, m, v, g in zip(weights, m, v, gradients, strict=True)]
        return tuple(one[which] for which in range(3) for one in new)

    return jax.shard_map(
        step,
        mesh=mesh,
        in_specs=(P(("rep", "dp"), None, None),) * 2 + (P(None, None, None),) * 9,
        out_specs=(P("rep", None, None),) * 9,
        check_vma=False,
    )
```

profile of v0, /device:TPU:112, one launch (start us, length us, event | category | flops | bytes accessed | tf_op | source)
XLA Modules:
  0.0 527.4 jit_solution(11005377456801113523)
XLA Ops:
  7.2 0.1 all-reduce.3.cloned.1.call-start
  7.3 6.3 %copy.20 = bf16[1,4096,512]{1,2,0:T(8,128)(2,1)} copy(bf16[1,4096,512]{2,1,0:T(8,128)(2,1)} %param.11) | data formatting | bytes 8388608 | tf_op args[0]
  13.6 3.2 fusion.15
  16.8 0.0 copy-start.17
  16.8 6.3 %copy.21 = bf16[1,4096,512]{1,2,0:T(8,128)(2,1)} copy(bf16[1,4096,512]{2,1,0:T(8,128)(2,1)} %param.12) | data formatting | bytes 8388608 | tf_op args[1]
  23.2 0.0 copy-done.5
  23.2 12.5 %convolution_convert_fusion.1 = bf16[4096,1664]{1,0:T(8,128)(2,1)} fusion(bf16[1,4096,512]{2,1,0:T(8,128)(2,1)} %param.12, bf16[2,1664,512]{2,1,0:T(8,128)(2,1)S(1)} %copy-done.5), kind=kOutput, calls=%fused_computation.23 | convolution fusion | flops 6986137600 | bytes 19529728 | tf_op jit(solution)/shard_map/transpose(jvp())/dot_general | solution.py:10
  35.7 0.0 copy-done.1
  35.7 0.0 copy-done.7
  35.7 13.0 %fusion.88 = f32[4096,1664]{1,0:T(8,128)} fusion(bf16[2,512,1664]{2,1,0:T(8,128)(2,1)S(1)} %copy-done.7, bf16[1,4096,512]{2,1,0:T(8,128)(2,1)S(1)} %copy-done.1, f32[4096]{0:T(1024)S(1)} %add_rsqrt_fusion), kind=kOutput, calls=%fused_computation.103 | convolution fusion | flops 6985613312 | bytes 33177600 | tf_op jit(solution)/shard_map/dot_general | solution.py:21
  48.7 0.0 copy-done.17
  48.7 27.4 %multiply_convert_fusion.1 = (bf16[4096,1664]{1,0:T(8,128)(2,1)}, f32[4096,1664]{1,0:T(8,128)}) fusion(f32[4096,1664]{1,0:T(8,128)} %fusion.88, bf16[2,512,1664]{2,1,0:T(8,128)(2,1)} %param.14, bf16[1,4096,512]{2,1,0:T(8,128)(2,1)} %param.11, f32[4096]{0:T(1024)S(1)} %add_rsqrt_fusion), kind=kOutput, calls=%fused_computation.17 | convolution fusion | flops 7026507776 | bytes 74072064 | tf_op jit(solution)/shard_map/dot_general | solution.py:22
  76.2 12.6 %fusion.19 = (f32[4096]{0:T(1024)S(1)}, bf16[4096,512]{0,1:T(8,128)(2,1)S(1)}) fusion(bf16[4096,1664]{1,0:T(8,128)(2,1)} %get-tuple-element.24, bf16[2,1664,512]{2,1,0:T(8,128)(2,1)S(1)} %copy-done.5, bf16[1,4096,512]{1,2,0:T(8,128)(2,1)} %copy.20), kind=kOutput, calls=%fused_computation.49 | convolution fusion | flops 6989803520 | bytes 23740416 | tf_op jit(solution)/shard_map/dot_general | solution.py:10
  88.7 0.0 copy-start.3
  88.8 0.0 copy-start.15
  88.8 2.0 copy-done.3
  90.8 0.0 copy-done.15
  90.8 0.0 copy-done.10
  90.8 13.0 %fusion.75 = f32[4096,1664]{1,0:T(8,128)} fusion(bf16[4096,512]{0,1:T(8,128)(2,1)S(1)} %get-tuple-element.27, f32[4096]{0:T(1024)S(1)} %fusion.101, bf16[2,512,1664]{2,1,0:T(8,128)(2,1)S(1)} %copy-done.10), kind=kOutput, calls=%fused_computation.92 | convolution fusion | flops 6985613312 | bytes 33177600 | tf_op jit(solution)/shard_map/jvp()/dot_general | solution.py:22
  103.8 34.4 %fusion.2 = (bf16[4096,1664]{1,0:T(8,128)(2,1)}, f32[4096,1664]{1,0:T(8,128)}) fusion(f32[4096,1664]{1,0:T(8,128)} %fusion.75, bf16[4096,1664]{1,0:T(8,128)(2,1)} %convolution_convert_fusion.1, bf16[2,512,1664]{2,1,0:T(8,128)(2,1)} %param.13, bf16[4096,512]{0,1:T(8,128)(2,1)} %copy-done.3, f32[4096]{0:T(1024)S(1)} %fusion.101), kind=kOutput, calls=%fused_computation.8 | convolution fusion | flops 7067402240 | bytes 87703552 | tf_op jit(solution)/shard_map/jvp()/dot_general | solution.py:21
  138.2 0.0 copy-done.2
  138.2 20.5 %fusion.59 = bf16[1,1664,512]{2,1,0:T(8,128)(2,1)} fusion(bf16[1,4096,512]{2,1,0:T(8,128)(2,1)S(1)} %copy-done.2, f32[4096,1664]{1,0:T(8,128)} %fusion.75, f32[4096,1664]{1,0:T(8,128)} %get-tuple-element.29), kind=kOutput, calls=%fused_computation.86 | convolution fusion | flops 7021068288 | bytes 60424192 | tf_op jit(solution)/shard_map/transpose(jvp())/dot_general | solution.py:10
  158.7 19.9 %fusion.63 = bf16[1,512,1664]{2,1,0:T(8,128)(2,1)} fusion(bf16[4096,1664]{1,0:T(8,128)(2,1)} %convolution_convert_fusion.1, bf16[4096,512]{0,1:T(8,128)(2,1)} %copy-done.3, f32[4096]{0:T(1024)S(1)} %fusion.101, f32[4096,1664]{1,0:T(8,128)} %get-tuple-element.29), kind=kOutput, calls=%fused_computation.88 | convolution fusion | flops 7027359744 | bytes 46809088 | tf_op jit(solution)/shard_map/transpose(jvp())/dot_general | solution.py:22
  178.6 0.0 copy-done.11
  178.6 19.0 %fusion.37 = bf16[4096,512]{0,1:T(8,128)(2,1)} fusion(bf16[4096,1664]{1,0:T(8,128)(2,1)} %convolution_convert_fusion.1, bf16[2,512,1664]{2,1,0:T(8,128)(2,1)S(1)} %copy-done.11, f32[4096,1664]{1,0:T(8,128)} %get-tuple-element.29), kind=kOutput, calls=%fused_computation.68 | convolution fusion | flops 7022313472 | bytes 46792704 | tf_op jit(solution)/shard_map/transpose(jvp())/dot_general | solution.py:22
  197.7 14.5 %fusion.69 = bf16[1,512,1664]{2,1,0:T(8,128)(2,1)} fusion(bf16[4096,1664]{1,0:T(8,128)(2,1)} %get-tuple-element.28, bf16[4096,512]{0,1:T(8,128)(2,1)} %copy-done.3, f32[4096]{0:T(1024)S(1)} %fusion.101), kind=kOutput, calls=%fused_computation.90 | convolution fusion | flops 6985613312 | bytes 19546112 | tf_op jit(solution)/shard_map/transpose(jvp())/dot_general | solution.py:21
  212.1 0.0 copy-done.4
  212.1 0.0 copy-done.8
  212.2 0.0 copy-start
  212.2 12.1 %fusion.21 = (f32[4096]{0:T(1024)S(1)}, bf16[4096,512]{0,1:T(8,128)(2,1)S(1)}) fusion(bf16[4096,512]{0,1:T(8,128)(2,1)S(1)} %copy-done.4, bf16[4096,512]{0,1:T(8,128)(2,1)} %fusion.37, bf16[4096,1664]{1,0:T(8,128)(2,1)} %get-tuple-element.28, bf16[2,512,1664]{2,1,0:T(8,128)(2,1)S(1)} %copy-done.8), kind=kOutput, calls=%fused_computation.51 | convolution fusion | flops 6989803520 | bytes 27934720 | tf_op jit(solution)/shard_map/transpose(jvp())/dot_general | solution.py:21
  224.3 0.0 copy-done.16
  224.3 0.0 copy-done
  224.3 3.1 fusion.42
  227.5 0.0 copy-start.6
  227.5 12.3 %fusion.62 = bf16[1,1664,512]{2,1,0:T(8,128)(2,1)} fusion(bf16[4096,1664]{1,0:T(8,128)(2,1)} %get-tuple-element.24, bf16[4096,512]{0,1:T(8,128)(2,1)S(1)} %fusion.42), kind=kOutput, calls=%fused_computation.87 | convolution fusion | flops 6980173824 | bytes 19529728 | tf_op jit(solution)/shard_map/transpose(jvp())/dot_general | solution.py:10
  239.8 0.0 copy-done.6
  239.8 10.8 %convolution_convert_fusion = bf16[4096,1664]{1,0:T(8,128)(2,1)} fusion(bf16[4096,512]{0,1:T(8,128)(2,1)S(1)} %fusion.42, bf16[2,1664,512]{2,1,0:T(8,128)(2,1)S(1)} %copy-done.6), kind=kOutput, calls=%fused_computation.22 | convolution fusion | flops 6986137600 | bytes 19529728 | tf_op jit(solution)/shard_map/transpose(jvp())/dot_general | solution.py:10
  250.7 20.0 %fusion.70 = bf16[1,512,1664]{2,1,0:T(8,128)(2,1)} fusion(bf16[4096,1664]{1,0:T(8,128)(2,1)} %convolution_convert_fusion, f32[4096,1664]{1,0:T(8,128)} %fusion.88, bf16[1,4096,512]{1,2,0:T(8,128)(2,1)} %copy.20, f32[4096]{0:T(1024)S(1)} %copy-done.18), kind=kOutput, calls=%fused_computation.91 | convolution fusion | flops 7027359744 | bytes 46809088 | tf_op jit(solution)/shard_map/transpose(jvp())/dot_general | solution.py:22
  270.7 26.8 %fusion.64 = bf16[1,512,1664]{2,1,0:T(8,128)(2,1)} fusion(f32[4096,1664]{1,0:T(8,128)} %fusion.88, f32[4096,1664]{1,0:T(8,128)} %get-tuple-element.25, bf16[4096,1664]{1,0:T(8,128)(2,1)} %convolution_convert_fusion, bf16[1,4096,512]{1,2,0:T(8,128)(2,1)} %copy.20, f32[4096]{0:T(1024)S(1)} %copy-done.18), kind=kOutput, calls=%fused_computation.89 | convolution fusion | flops 7061438464 | bytes 74072064 | tf_op jit(solution)/shard_map/transpose(jvp())/dot_general | solution.py:21
  297.5 0.1 all-reduce.3.cloned.1.call-update
  297.6 184.5 %all-reduce.3.cloned.1.call-done = (bf16[1,512,1664]{2,1,0:T(8,128)(2,1)}, bf16[1,512,1664]{2,1,0:T(8,128)(2,1)}, bf16[1,512,1664]{2,1,0:T(8,128)(2,1)}, bf16[1,...) async-done(((bf16[1,512,1664]{2,1,0:T(8,128)(2,1)}, bf16[1,512,1664]{2,1,0:T(8,128)(2,1)}, bf16[1,512,1664]{2,1,0:T(8,128)(2,1)}, ...) | async-done | bytes 10223632 | tf_op jit(solution)/shard_map/psum | solution.py:45
  482.1 14.3 %fusion.32 = (bf16[2,1664,512]{2,1,0:T(8,128)(2,1)}, f32[2,1664,512]{2,1,0:T(8,128)}, f32[2,1664,512]{2,1,0:T(8,128)}) fusion(bf16[2,1664,512]{2,1,0:T(8,128)(2,1)} %param.15, bf16[1,1664,512]{2,1,0:T(8,128)(2,1)} %get-tuple-element.13, bf16[1,1664,512]{2,1,0:T(8,128)(2,1)} %get-tuple-element.14, f32[2,1664,512]{2,1,0:T(8,128)} %param.21, ...), kind=kLoop, calls=%fused_computation.63 | loop fusion | flops 32374784 | bytes 37486592 | tf_op jit(solution)/shard_map/convert_element_type | solution.py:30
  496.4 0.0 slice-done.1
  496.4 0.0 copy-done.9
  496.4 1.6 copy-done.12
  498.0 0.5 copy-done.13
  498.5 0.5 copy-done.14
  498.9 21.2 %fusion.24 = (bf16[2,512,1664]{2,1,0:T(8,128)(2,1)}, f32[2,512,1664]{2,1,0:T(8,128)}, f32[2,512,1664]{2,1,0:T(8,128)}, bf16[2,512,1664]{2,1,0:T(8,128)(2,1)}, f3...) fusion(bf16[2,512,1664]{2,1,0:T(8,128)(2,1)S(1)} %copy-done.9, bf16[1,512,1664]{2,1,0:T(8,128)(2,1)S(1)} %copy-done.13, ...), kind=kLoop, calls=%fused_computation.55 | loop fusion | flops 64749568 | bytes 74973184 | tf_op jit(solution)/shard_map/convert_element_type | solution.py:30
  (22 shorter events, 0.1 us)
Async XLA Ops:
  7.2 474.9 %all-reduce.3.cloned.1.call-start = ((), (), s32[]{:S(2)}) async-start(), calls=%async_computation | async-start | bytes 20447232 | tf_op jit(solution)/shard_map/psum | solution.py:45
  13.6 9.6 %copy-start.5 = (bf16[2,1664,512]{2,1,0:T(8,128)(2,1)S(1)}, bf16[2,1664,512]{2,1,0:T(8,128)(2,1)}, u32[]{:S(2)}) copy-start(bf16[2,1664,512]{2,1,0:T(8,128)(2,1)} %param.15) | copy-start | bytes 10223620
  16.8 31.9 %copy-start.17 = (f32[4096]{0:T(1024)}, f32[4096]{0:T(1024)S(1)}, u32[]{:S(2)}) copy-start(f32[4096]{0:T(1024)S(1)} %add_rsqrt_fusion) | copy-start | bytes 49156
  23.2 12.6 %copy-start.1 = (bf16[1,4096,512]{2,1,0:T(8,128)(2,1)S(1)}, bf16[1,4096,512]{2,1,0:T(8,128)(2,1)}, u32[]{:S(2)}) copy-start(bf16[1,4096,512]{2,1,0:T(8,128)(2,1)} %param.11) | copy-start | bytes 12582916
  23.2 12.6 %copy-start.7 = (bf16[2,512,1664]{2,1,0:T(8,128)(2,1)S(1)}, bf16[2,512,1664]{2,1,0:T(8,128)(2,1)}, u32[]{:S(2)}) copy-start(bf16[2,512,1664]{2,1,0:T(8,128)(2,1)} %param.13) | copy-start | bytes 10223620
  76.2 14.6 %copy-start.10 = (bf16[2,512,1664]{2,1,0:T(8,128)(2,1)S(1)}, bf16[2,512,1664]{2,1,0:T(8,128)(2,1)}, u32[]{:S(2)}) copy-start(bf16[2,512,1664]{2,1,0:T(8,128)(2,1)} %param.14) | copy-start | bytes 10223620
  88.7 2.0 copy-start.3
  88.8 2.0 copy-start.15
  103.8 34.4 %copy-start.2 = (bf16[1,4096,512]{2,1,0:T(8,128)(2,1)S(1)}, bf16[1,4096,512]{2,1,0:T(8,128)(2,1)}, u32[]{:S(2)}) copy-start(bf16[1,4096,512]{2,1,0:T(8,128)(2,1)} %param.12) | copy-start | bytes 12582916
  158.7 19.9 %copy-start.11 = (bf16[2,512,1664]{2,1,0:T(8,128)(2,1)S(1)}, bf16[2,512,1664]{2,1,0:T(8,128)(2,1)}, u32[]{:S(2)}) copy-start(bf16[2,512,1664]{2,1,0:T(8,128)(2,1)} %param.14) | copy-start | bytes 10223620
  197.7 14.5 %copy-start.4 = (bf16[4096,512]{0,1:T(8,128)(2,1)S(1)}, bf16[4096,512]{0,1:T(8,128)(2,1)}, u32[]{:S(2)}) copy-start(bf16[4096,512]{0,1:T(8,128)(2,1)} %copy-done.3) | copy-start | bytes 12582916
  197.7 14.5 %copy-start.8 = (bf16[2,512,1664]{2,1,0:T(8,128)(2,1)S(1)}, bf16[2,512,1664]{2,1,0:T(8,128)(2,1)}, u32[]{:S(2)}) copy-start(bf16[2,512,1664]{2,1,0:T(8,128)(2,1)} %param.13) | copy-start | bytes 10223620
  212.1 12.2 %copy-start.16 = (f32[4096]{0:T(1024)S(1)}, f32[4096]{0:T(1024)}, u32[]{:S(2)}) copy-start(f32[4096]{0:T(1024)} %copy-done.15) | copy-start | bytes 49156
  212.2 12.2 %copy-start = (bf16[1,4096,512]{1,2,0:T(8,128)(2,1)S(1)}, bf16[1,4096,512]{1,2,0:T(8,128)(2,1)}, u32[]{:S(2)}) copy-start(bf16[1,4096,512]{1,2,0:T(8,128)(2,1)} %copy.21) | copy-start | bytes 12582916
  227.5 12.3 %copy-start.6 = (bf16[2,1664,512]{2,1,0:T(8,128)(2,1)S(1)}, bf16[2,1664,512]{2,1,0:T(8,128)(2,1)}, u32[]{:S(2)}) copy-start(bf16[2,1664,512]{2,1,0:T(8,128)(2,1)} %param.15) | copy-start | bytes 10223620
  239.8 10.9 %copy-start.18 = (f32[4096]{0:T(1024)S(1)}, f32[4096]{0:T(1024)}, u32[]{:S(2)}) copy-start(f32[4096]{0:T(1024)} %copy-done.17) | copy-start | bytes 49156
  297.5 198.9 %slice-start = ((s8[6815744]{0:T(1024)(128)(4,1)}), s8[2621440]{0:T(1024)(128)(4,1)S(1)}, s32[]{:S(2)}) async-start(s8[6815744]{0:T(1024)(128)(4,1)} %bitcast.82), calls=%async_computation.1 | async-start | bytes 5242880
  482.1 14.4 %slice-start.1 = ((s8[6815744]{0:T(1024)(128)(4,1)}), s8[4194304]{0:T(1024)(128)(4,1)S(1)}, s32[]{:S(2)}) async-start(s8[6815744]{0:T(1024)(128)(4,1)} %bitcast.82), calls=%async_computation.2 | async-start | bytes 8388608
  482.1 14.4 %copy-start.9 = (bf16[2,512,1664]{2,1,0:T(8,128)(2,1)S(1)}, bf16[2,512,1664]{2,1,0:T(8,128)(2,1)}, u32[]{:S(2)}) copy-start(bf16[2,512,1664]{2,1,0:T(8,128)(2,1)} %param.13) | copy-start | bytes 10223620
  482.1 15.9 %copy-start.12 = (bf16[2,512,1664]{2,1,0:T(8,128)(2,1)S(1)}, bf16[2,512,1664]{2,1,0:T(8,128)(2,1)}, u32[]{:S(2)}) copy-start(bf16[2,512,1664]{2,1,0:T(8,128)(2,1)} %param.14) | copy-start | bytes 10223620
  482.1 16.4 %copy-start.13 = (bf16[1,512,1664]{2,1,0:T(8,128)(2,1)S(1)}, bf16[1,512,1664]{2,1,0:T(8,128)(2,1)}, u32[]{:S(2)}) copy-start(bf16[1,512,1664]{2,1,0:T(8,128)(2,1)} %get-tuple-element.9) | copy-start | bytes 5111812
  482.1 16.9 %copy-start.14 = (bf16[1,512,1664]{2,1,0:T(8,128)(2,1)S(1)}, bf16[1,512,1664]{2,1,0:T(8,128)(2,1)}, u32[]{:S(2)}) copy-start(bf16[1,512,1664]{2,1,0:T(8,128)(2,1)} %get-tuple-element.10) | copy-start | bytes 5111812
Sparse Core Ops, SparseCore 0:
  297.7 184.3 all-reduce.2
where the time goes:
time: 535 us; the launch traced here: 527 us
  matrix products  269 us (50%)
  waiting for transfers between devices  185 us (35%)
  other arithmetic  41.9 us (8%)
  local copies, waits for them, and re-layouts  17.2 us (3%)
  between operations  14.7 us (3%)
    psum x1, waiting for transfers between devices, step(): summed[number] = [lax.psum(by_w[name], 'dp') for name in NAMES]  184 us
    dot_general x5, matrix products, layer(): gate = jnp.dot(a, w['w_gate'], preferred_element_type=jnp.float32)  101 us
    dot_general x5, matrix products, layer(): up = jnp.dot(a, w['w_up'], preferred_element_type=jnp.float32)  99.4 us
    dot_general x5, matrix products, matmul(): jnp.dot(a, w, preferred_element_type=jnp.float32).astype(jnp.bfloat16)  68.8 us
    convert_element_type x2, other arithmetic, adamw(): return ((w - 0.02 * step).astype(jnp.bfloat16), m, v)  35.5 us
    unnamed x44, local copies, waits for them, and re-layouts  17.2 us
  transfers between devices with their start and end apart: 1, of which 1 were waited for; matrix products, arithmetic and copies ran while one was open for 0% of the time, Pallas kernels for 0%

commit v1 on v0

v1 whole, which is shorter than its diff:
```python
import functools

import jax
import jax.numpy as jnp
from jax import lax
from jax.experimental import pallas as pl
from jax.experimental.pallas import tpu as pltpu
from jax.sharding import PartitionSpec as P

BF16, F32 = jnp.bfloat16, jnp.float32
WIDE = 256
LANES = 128
TILE = 1024
ROWS = 512


def at(index, size):
    if isinstance(index, int):
        return pl.ds(index * size, size)
    return pl.ds(pl.multiple_of(index * size, size), size)


def dot(a, b):
    return jnp.dot(a, b, preferred_element_type=F32)


def dot_t(a, b):
    return lax.dot_general(a, b, (((1,), (1,)), ((), ())), preferred_element_type=F32)


def scale_of(wide):
    return lax.rsqrt(jnp.mean(wide * wide, -1, keepdims=True) + 1e-6)


def normed(h):
    wide = h.astype(F32)
    return (wide * scale_of(wide)).astype(BF16)


def main_kernel(x_hbm, dy_hbm, wg_hbm, wu_hbm, wd_hbm, out_hbm, h_ref, a_ref, at_ref, g_ref, gt_ref, da_ref, wgu_ref, wd_ref, mid_ref, hid_ref, dgu_ref, term_ref, w_sem, x_sem, dy_sem, out_sem):
    tokens, d = h_ref.shape
    layers, ff, _ = wd_ref.shape
    full = ff // WIDE
    widths = [WIDE] * full + ([ff % WIDE] if ff % WIDE else [])

    def weight_copies(layer):
        copies = []
        for k, width in enumerate(widths):
            for source, offset in ((wg_hbm, 0), (wu_hbm, width)):
                copies.append((source.at[layer, :, pl.ds(k * WIDE, width)], wgu_ref.at[layer, :, pl.ds(2 * k * WIDE + offset, width)]))
        copies.append((wd_hbm.at[layer], wd_ref.at[layer]))
        return [pltpu.make_async_copy(source, target, w_sem.at[layer, i]) for i, (source, target) in enumerate(copies)]

    def x_copy(t, target):
        return pltpu.make_async_copy(x_hbm.at[0, at(t, ROWS)], target.at[at(t, ROWS)], x_sem.at[t])

    dy_copy = pltpu.make_async_copy(dy_hbm.at[0], g_ref, dy_sem)
    steps = tokens // ROWS
    for copy in weight_copies(0):
        copy.start()
    for t in range(steps):
        x_copy(t, h_ref).start()
    dy_copy.start()
    for layer in range(1, layers):
        for copy in weight_copies(layer):
            copy.start()
    for copy in weight_copies(0):
        copy.wait()

    def forward(t, carry):
        rows = at(t, ROWS)
        x_copy(t, h_ref).wait()
        x = h_ref[rows, :]
        a = normed(x)
        for k, width in enumerate(widths):
            gu = dot(a, wgu_ref[0, :, pl.ds(2 * k * WIDE, 2 * width)])
            gate, up = gu[:, :width], gu[:, width:]
            mid_ref[:, pl.ds(k * WIDE, width)] = (gate * jax.nn.sigmoid(gate) * up).astype(BF16)
        h = (x.astype(F32) + dot(mid_ref[...], wd_ref[0]).astype(BF16).astype(F32)).astype(BF16)
        h_ref[rows, :] = h
        a = normed(h)
        a_ref[rows, :] = a
        at_ref[:, rows] = a.T
        return carry

    lax.fori_loop(0, steps, forward, 0)
    dy_copy.wait()

    def turn(t, carry):
        rows = at(t, ROWS)
        gt_ref[:, rows] = g_ref[rows, :].T
        return carry

    lax.fori_loop(0, steps, turn, 0)
    for layer in range(1, layers):
        for copy in weight_copies(layer):
            copy.wait()

    def chunk(layer, k, width, first, last):
        gu_cols = pl.ds(pl.multiple_of(k * 2 * WIDE, 2 * WIDE), 2 * width)
        down_rows = pl.ds(pl.multiple_of(k * WIDE, WIDE), width)

        def hidden(t, carry):
            rows = at(t, TILE)
            gu = dot(a_ref[rows, :], wgu_ref[layer, :, gu_cols])
            dh = dot_t(g_ref[rows, :], wd_ref[layer, down_rows, :]).astype(BF16).astype(F32)
            gate, up = gu[:, :width], gu[:, width:]
            s = jax.nn.sigmoid(gate)
            silu = gate * s
            hid_ref[rows, pl.ds(0, width)] = (silu * up).astype(BF16)
            dgu_ref[rows, pl.ds(width, width)] = (dh * silu).astype(BF16)
            dgu_ref[rows, pl.ds(0, width)] = (dh * up * (s + silu * (1.0 - s))).astype(BF16)
            return carry

        lax.fori_loop(0, tokens // TILE, hidden, 0)
        dgu = dot(at_ref[...], dgu_ref[:, pl.ds(0, 2 * width)]).astype(BF16)
        down = dot(gt_ref[...], hid_ref[:, pl.ds(0, width)]).astype(BF16)
        for j in range(width // LANES):
            for i, piece in enumerate((dgu[:, j * LANES : (j + 1) * LANES], dgu[:, width + j * LANES : width + (j + 1) * LANES], down[:, j * LANES : (j + 1) * LANES])):
                term_ref[:, pl.ds(pl.multiple_of(k * 3 * WIDE, 3 * WIDE) + (3 * j + i) * LANES, LANES)] = piece
        if layer:

            def by_a(t, carry):
                rows = at(t, TILE)
                part = dot_t(dgu_ref[rows, pl.ds(0, 2 * width)], wgu_ref[layer, :, gu_cols])
                if first is True:
                    da_ref[rows, :] = part
                else:
                    da_ref[rows, :] += part
                return carry

            lax.fori_loop(0, tokens // TILE, by_a, 0)

    def backward(layer):
        if layer:
            chunk(layer, 0, WIDE, True, False)

            def body(k, carry):
                chunk(layer, k, WIDE, False, False)
                return carry

            lax.fori_loop(1, full, body, 0)
        else:

            def body(k, carry):
                chunk(layer, k, WIDE, False, False)
                return carry

            lax.fori_loop(0, full, body, 0)
        for k in range(full, len(widths)):
            chunk(layer, k, widths[k], False, True)
        copy = pltpu.make_async_copy(term_ref, out_hbm.at[layer], out_sem)
        copy.start()
        copy.wait()

    backward(1)

    for t in range(steps):
        x_copy(t, a_ref).start()

    def between(t, carry):
        rows = at(t, ROWS)
        x_copy(t, a_ref).wait()
        da = da_ref[rows, :].astype(BF16).astype(F32)
        h = h_ref[rows, :].astype(F32)
        r = scale_of(h)
        inner = jnp.mean(da * h, -1, keepdims=True)
        dh = (r * (da - h * (r * r * inner))).astype(BF16).astype(F32)
        g = (g_ref[rows, :].astype(F32) + dh).astype(BF16)
        g_ref[rows, :] = g
        gt_ref[:, rows] = g.T
        a = normed(a_ref[rows, :])
        a_ref[rows, :] = a
        at_ref[:, rows] = a.T
        return carry

    lax.fori_loop(0, steps, between, 0)
    backward(0)


def main_call(x, dy, wg, wu, wd):
    layers, d, ff = wg.shape
    tokens = x.shape[1]
    pieces = 2 * -(-ff // WIDE) + 1
    any_ = pl.BlockSpec(memory_space=pl.ANY)
    return pl.pallas_call(
        main_kernel,
        out_shape=jax.ShapeDtypeStruct((layers, d, 3 * ff), BF16),
        in_specs=[any_] * 5,
        out_specs=any_,
        scratch_shapes=[
            pltpu.VMEM((tokens, d), BF16),
            pltpu.VMEM((tokens, d), BF16),
            pltpu.VMEM((d, tokens), BF16),
            pltpu.VMEM((tokens, d), BF16),
            pltpu.VMEM((d, tokens), BF16),
            pltpu.VMEM((tokens, d), F32),
            pltpu.VMEM((layers, d, 2 * ff), BF16),
            pltpu.VMEM((layers, ff, d), BF16),
            pltpu.VMEM((ROWS, ff), BF16),
            pltpu.VMEM((tokens, WIDE), BF16),
            pltpu.VMEM((tokens, 2 * WIDE), BF16),
            pltpu.VMEM((d, 3 * ff), BF16),
            pltpu.SemaphoreType.DMA((layers, pieces)),
            pltpu.SemaphoreType.DMA((tokens // ROWS,)),
            pltpu.SemaphoreType.DMA,
            pltpu.SemaphoreType.DMA,
        ],
        compiler_params=pltpu.CompilerParams(vmem_limit_bytes=67_000_000),
        name="main",
    )(x, dy, wg, wu, wd)


def adamw(w, m, v, g):
    m = 0.9 * m + 0.1 * g
    v = 0.95 * v + 0.05 * g * g
    step = m * lax.rsqrt(v + 1e-8) + 0.1 * w
    return (w - 0.02 * step).astype(BF16), m, v


def adam_kernel(which, g_ref, *refs):
    ins, outs = refs[:9], refs[-9:]
    ff = ins[0].shape[-1]
    for j in range(ff // LANES):
        cols = pl.ds(j * LANES, LANES)
        for i in range(3):
            g = g_ref[0, :, pl.ds((3 * j + i) * LANES, LANES)].astype(F32)
            index = (0, slice(None), cols)
            if i == 2:
                g, index = g.T, (0, cols, slice(None))
            w, m, v = adamw(ins[i][index].astype(F32), ins[3 + i][index], ins[6 + i][index], g)
            outs[i][index], outs[3 + i][index], outs[6 + i][index] = w, m, v


def adam_call(g, arrays):
    layers, d, ff = arrays[0].shape
    row = pl.BlockSpec((1, LANES, ff), lambda l, r, s: (l, r, 0))
    column = pl.BlockSpec((1, ff, LANES), lambda l, r, s: (l, 0, r))
    specs = [row, row, column] * 3
    return pl.pallas_call(
        adam_kernel,
        grid_spec=pltpu.PrefetchScalarGridSpec(
            num_scalar_prefetch=1,
            grid=(layers, d // LANES),
            in_specs=[pl.BlockSpec((1, LANES, 3 * ff), lambda l, r, s: (l, r, 0))] + specs,
            out_specs=specs,
        ),
        out_shape=[jax.ShapeDtypeStruct(a.shape, a.dtype) for a in arrays],
        compiler_params=pltpu.CompilerParams(vmem_limit_bytes=60_000_000),
        name="adam",
    )(jnp.zeros((1,), jnp.int32), g, *arrays)


def solution(mesh):
    def step(x, dy, *arrays):
        g = main_call(x, dy, *arrays[:3])
        g = lax.psum(g, "dp")
        return tuple(adam_call(g, arrays))

    return jax.shard_map(
        step,
        mesh=mesh,
        in_specs=(P(("rep", "dp"), None, None),) * 2 + (P(None, None, None),) * 9,
        out_specs=(P("rep", None, None),) * 9,
        check_vma=False,
    )
```

time: 535 us -> 403 us (0.75); the launches traced: 527 us -> 403 us
  matrix products: 269 us -> 0 us
  Pallas kernels: 0 us -> 204 us
  other arithmetic: 41.9 us -> 0 us
  local copies, waits for them, and re-layouts: 17.2 us -> 0 us
    dot_general x15 -> x0, matrix products: 269 us -> none  [the longest x5 101 us: layer(): gate = jnp.dot(a, w['w_gate'], preferred_element_type=jnp.float32)]
    pallas_call x0 -> x2, Pallas kernels: none -> 204 us  [the longest x1 167 us: main_call(): pl.pallas_call(main_kernel, out_shape=jax.ShapeDtypeStruct((layers, d, 3...]
    convert_element_type x2 -> x0, other arithmetic: 35.5 us -> none  [adamw(): return ((w - 0.02 * step).astype(jnp.bfloat16), m, v)]
    unnamed x44 -> x0, local copies, waits for them, and re-layouts: 17.2 us -> none
where the time goes in v1:
time: 403 us
  Pallas kernels  204 us (51%)
  waiting for transfers between devices  185 us (46%)
  between operations  14.1 us (3%)
    psum x1, waiting for transfers between devices, step(): g = lax.psum(g, 'dp')  184 us
    pallas_call x1, Pallas kernels, main_call(): pl.pallas_call(main_kernel, out_shape=jax.ShapeDtypeStruct((layers, d, 3...  167 us
    pallas_call x1, Pallas kernels, adam_call(): pl.pallas_call(adam_kernel, grid_spec=pltpu.PrefetchScalarGridSpec(num_sc...  37.3 us
  transfers between devices with their start and end apart: 1, of which 1 were waited for; matrix products, arithmetic and copies ran while one was open for 0% of the time, Pallas kernels for 0%

profile of v1, /device:TPU:112, one launch (start us, length us, event | category | flops | bytes accessed | tf_op | source)
XLA Modules:
  0.0 402.6 jit_solution(8585376799435127748)
XLA Ops:
  7.2 0.1 all-reduce.2.cloned.1.call-start
  7.3 166.6 %main.1 = bf16[2,512,4992]{2,1,0:T(8,128)(2,1)} custom-call(bf16[1,4096,512]{2,1,0:T(8,128)(2,1)} %x_hbm.1, bf16[1,4096,512]{2,1,0:T(8,128)(2,1)} %dy_hbm.1, bf16[2,512,1664]{2,1,0:T(8,128)(2,1)} %refs_0_.1, bf16[2,512,1664]{2,1,0:T(8,128)(2,1)} %refs_1_.1, bf16[2,1664,512]{2,1,0:T(8,128)(2,1)} %refs_2_.1), custom_call_target="tpu_custom_call" | custom-call | tf_op jit(solution)/shard_map/main/pallas_call | solution.py:186
  173.8 0.1 all-reduce.2.cloned.1.call-update
  173.9 184.4 %all-reduce.2.cloned.1.call-done.g_ref = bf16[2,512,4992]{2,1,0:T(8,128)(2,1)} async-done(((bf16[2,512,4992]{2,1,0:T(8,128)(2,1)}), bf16[2,512,4992]{2,1,0:T(8,128)(2,1)}) %all-reduce.2.cloned.1.call-update) | async-done | bytes 10223632 | tf_op jit(solution)/shard_map/psum | solution.py:257
  358.3 37.3 %adam.1 = (bf16[2,512,1664]{2,1,0:T(8,128)(2,1)}, bf16[2,512,1664]{2,1,0:T(8,128)(2,1)}, bf16[2,1664,512]{2,1,0:T(8,128)(2,1)}, f32[2,512,1664]{2,1,0:T(8,128)},...) custom-call(s32[1]{0:T(128)} %constant.0.clone.1.which, ...), custom_call_target="tpu_custom_call" | custom-call | tf_op jit(solution)/shard_map/adam/pallas_call | solution.py:240
Async XLA Ops:
  7.2 351.2 %all-reduce.2.cloned.1.call-start = ((), (), s32[]{:S(2)}) async-start(), calls=%async_computation | async-start | bytes 20447232 | tf_op jit(solution)/shard_map/psum | solution.py:257
Sparse Core Ops, SparseCore 0:
  174.0 184.2 all-reduce.1

commit v2 on v1

--- a/solution.py
+++ b/solution.py
@@ -37,11 +37,104 @@
     return (wide * scale_of(wide)).astype(BF16)
 
 
-def main_kernel(x_hbm, dy_hbm, wg_hbm, wu_hbm, wd_hbm, out_hbm, h_ref, a_ref, at_ref, g_ref, gt_ref, da_ref, wgu_ref, wd_ref, mid_ref, hid_ref, dgu_ref, term_ref, w_sem, x_sem, dy_sem, out_sem):
+def main_kernel(
+    n, x_hbm, dy_hbm, wg_hbm, wu_hbm, wd_hbm,
+    all_hbm, own_hbm,
+    h_ref, a_ref, at_ref, g_ref, gt_ref, da_ref, wgu_ref, wd_ref, mid_ref, hid_ref, dgu_ref, term_ref, one_ref, two_ref,
+    w_sem, x_sem, dy_sem, one_send, one_recv, two_send, two_recv, near_send, near_recv, far_send, far_recv, keep_sem,
+):
     tokens, d = h_ref.shape
     layers, ff, _ = wd_ref.shape
     full = ff // WIDE
     widths = [WIDE] * full + ([ff % WIDE] if ff % WIDE else [])
+    share = d // n
+    half = share // 2
+    me = lax.axis_index("dp")
+    right, left, across = (lax.rem(me + i, n) for i in (1, n - 1, 2))
+    ways = (right, left)
+
+    barrier = pltpu.get_barrier_semaphore()
+    for way in ways:
+        pl.semaphore_signal(barrier, inc=1, device_id={"dp": way}, device_id_type=pl.DeviceIdType.MESH)
+
+    def cols_of(k):
+        return pl.ds(pl.multiple_of(k * 3 * WIDE, 3 * WIDE), 3 * widths[k] if isinstance(k, int) else 3 * WIDE)
+
+    def rows_of(owner, part=None):
+        if part is None:
+            return pl.ds(pl.multiple_of(owner * share, share), share)
+        return pl.ds(pl.multiple_of(owner * share + part * half, half), half)
+
+    def remote(source, target, send, recv, way):
+        return pltpu.make_async_remote_copy(
+            src_ref=source, dst_ref=target, send_sem=send, recv_sem=recv, device_id={"dp": ways[way]}, device_id_type=pl.DeviceIdType.MESH
+        )
+
+    def one(layer, k, way):
+        cols = cols_of(k)
+        return remote(term_ref.at[rows_of(across, way), cols], one_ref.at[way, :, cols], one_send.at[layer, k, way], one_recv.at[layer, k, way], way)
+
+    def two(layer, k, way):
+        cols = cols_of(k)
+        return remote(term_ref.at[rows_of(ways[way]), cols], two_ref.at[way, :, cols], two_send.at[layer, k, way], two_recv.at[layer, k, way], way)
+
+    def near(k, way):
+        cols = cols_of(k)
+        return remote(term_ref.at[rows_of(me), cols], all_hbm.at[rows_of(me), cols], near_send.at[k, way], near_recv.at[k, way], way)
+
+    def far(k, way):
+        cols = cols_of(k)
+        block = all_hbm.at[rows_of(ways[1 - way], way), cols]
+        return remote(block, block, far_send.at[k, way], far_recv.at[k, way], way)
+
+    def keep(layer, k):
+        cols = cols_of(k)
+        target = all_hbm.at[rows_of(me), cols] if layer else own_hbm.at[:, cols]
+        return pltpu.make_async_copy(term_ref.at[rows_of(me), cols], target, keep_sem.at[layer, k])
+
+    def start_one(layer, k):
+        for way in range(2):
+            one(layer, k, way).start()
+
+    def start_two(layer, k):
+        cols = cols_of(k)
+        for way in range(2):
+            one(layer, k, way).wait()
+            rows = rows_of(ways[way], way)
+            term_ref[rows, cols] = (term_ref[rows, cols].astype(F32) + one_ref[way, :, cols].astype(F32)).astype(BF16)
+        for way in range(2):
+            two(layer, k, way).start()
+
+    def finish(layer, k):
+        cols = cols_of(k)
+        rows = rows_of(me)
+        for way in range(2):
+            two(layer, k, way).wait()
+        term_ref[rows, cols] = (term_ref[rows, cols].astype(F32) + two_ref[0, :, cols].astype(F32) + two_ref[1, :, cols].astype(F32)).astype(BF16)
+        if layer:
+            for way in range(2):
+                near(k, way).start()
+        keep(layer, k).start()
+
+    def start_far(k):
+        for way in range(2):
+            near(k, way).wait()
+        keep(1, k).wait()
+        for way in range(2):
+            far(k, way).start()
+
+    def when(condition, action, *args):
+        if isinstance(condition, bool):
+            if condition:
+                action(*args)
+        else:
+            pl.when(condition)(lambda: action(*args))
+
+    def meanwhile(layer, k):
+        when(k >= 2, finish, layer, k - 2)
+        when(k >= 1, start_two, layer, k - 1)
+        if not layer:
+            start_far(k)
 
     def weight_copies(layer):
         copies = []
@@ -113,11 +206,13 @@
             return carry
 
         lax.fori_loop(0, tokens // TILE, hidden, 0)
+        meanwhile(layer, k)
         dgu = dot(at_ref[...], dgu_ref[:, pl.ds(0, 2 * width)]).astype(BF16)
         down = dot(gt_ref[...], hid_ref[:, pl.ds(0, width)]).astype(BF16)
         for j in range(width // LANES):
             for i, piece in enumerate((dgu[:, j * LANES : (j + 1) * LANES], dgu[:, width + j * LANES : width + (j + 1) * LANES], down[:, j * LANES : (j + 1) * LANES])):
                 term_ref[:, pl.ds(pl.multiple_of(k * 3 * WIDE, 3 * WIDE) + (3 * j + i) * LANES, LANES)] = piece
+        start_one(layer, k)
         if layer:
 
             def by_a(t, carry):
@@ -149,11 +244,12 @@
             lax.fori_loop(0, full, body, 0)
         for k in range(full, len(widths)):
             chunk(layer, k, widths[k], False, True)
-        copy = pltpu.make_async_copy(term_ref, out_hbm.at[layer], out_sem)
-        copy.start()
-        copy.wait()
-
+
+    last = len(widths) - 1
+    pl.semaphore_wait(barrier, 2)
     backward(1)
+    finish(1, last - 1)
+    start_two(1, last)
 
     for t in range(steps):
         x_copy(t, a_ref).start()
@@ -175,19 +271,31 @@
         return carry
 
     lax.fori_loop(0, steps, between, 0)
+    finish(1, last)
     backward(0)
-
-
-def main_call(x, dy, wg, wu, wd):
+    finish(0, last - 1)
+    start_two(0, last)
+    finish(0, last)
+    for k in range(len(widths)):
+        keep(0, k).wait()
+        for way in range(2):
+            far(k, way).wait()
+
+
+def main_call(n, x, dy, wg, wu, wd):
     layers, d, ff = wg.shape
     tokens = x.shape[1]
-    pieces = 2 * -(-ff // WIDE) + 1
+    if layers != 2 or n != 4:
+        raise ValueError("unsupported sizes")
+    chunks = -(-ff // WIDE)
     any_ = pl.BlockSpec(memory_space=pl.ANY)
+    share = d // n
+    sems = pltpu.SemaphoreType.DMA
     return pl.pallas_call(
-        main_kernel,
-        out_shape=jax.ShapeDtypeStruct((layers, d, 3 * ff), BF16),
+        functools.partial(main_kernel, n),
+        out_shape=[jax.ShapeDtypeStruct((d, 3 * ff), BF16), jax.ShapeDtypeStruct((share, 3 * ff), BF16)],
         in_specs=[any_] * 5,
-        out_specs=any_,
+        out_specs=[any_] * 2,
         scratch_shapes=[
             pltpu.VMEM((tokens, d), BF16),
             pltpu.VMEM((tokens, d), BF16),
@@ -201,12 +309,16 @@
             pltpu.VMEM((tokens, WIDE), BF16),
             pltpu.VMEM((tokens, 2 * WIDE), BF16),
             pltpu.VMEM((d, 3 * ff), BF16),
-            pltpu.SemaphoreType.DMA((layers, pieces)),
-            pltpu.SemaphoreType.DMA((tokens // ROWS,)),
-            pltpu.SemaphoreType.DMA,
-            pltpu.SemaphoreType.DMA,
+            pltpu.VMEM((2, share // 2, 3 * ff), BF16),
+            pltpu.VMEM((2, share, 3 * ff), BF16),
+            sems((layers, 2 * chunks + 1)),
+            sems((tokens // ROWS,)),
+            sems,
+            *[sems((layers, chunks, 2))] * 4,
+            *[sems((chunks, 2))] * 4,
+            sems((layers, chunks)),
         ],
-        compiler_params=pltpu.CompilerParams(vmem_limit_bytes=67_000_000),
+        compiler_params=pltpu.CompilerParams(vmem_limit_bytes=67_000_000, collective_id=0, has_side_effects=True),
         name="main",
     )(x, dy, wg, wu, wd)
 
@@ -218,44 +330,82 @@
     return (w - 0.02 * step).astype(BF16), m, v
 
 
-def adam_kernel(which, g_ref, *refs):
-    ins, outs = refs[:9], refs[-9:]
+def adam_kernel(sources, where, *refs):
+    count = sum(parts for _, parts in sources)
+    ins, outs = refs[count : count + 9], refs[-9:]
     ff = ins[0].shape[-1]
-    for j in range(ff // LANES):
-        cols = pl.ds(j * LANES, LANES)
-        for i in range(3):
-            g = g_ref[0, :, pl.ds((3 * j + i) * LANES, LANES)].astype(F32)
-            index = (0, slice(None), cols)
-            if i == 2:
-                g, index = g.T, (0, cols, slice(None))
-            w, m, v = adamw(ins[i][index].astype(F32), ins[3 + i][index], ins[6 + i][index], g)
-            outs[i][index], outs[3 + i][index], outs[6 + i][index] = w, m, v
-
-
-def adam_call(g, arrays):
+    start = 0
+    for steps, parts in sources:
+        mine, refs = refs[:parts], refs[parts:]
+
+        @pl.when((pl.program_id(0) >= start) & (pl.program_id(0) < start + steps))
+        def _(mine=mine):
+            for j in range(ff // LANES):
+                cols = pl.ds(j * LANES, LANES)
+                for i in range(3):
+                    g = [ref[:, pl.ds((3 * j + i) * LANES, LANES)].astype(F32) for ref in mine]
+                    g = jnp.concatenate(g, 0) if len(g) > 1 else g[0]
+                    index = (0, slice(None), cols)
+                    if i == 2:
+                        g, index = g.T, (0, cols, slice(None))
+                    w, m, v = adamw(ins[i][index].astype(F32), ins[3 + i][index], ins[6 + i][index], g)
+                    outs[i][index], outs[3 + i][index], outs[6 + i][index] = w, m, v
+
+        start += steps
+
+
+def adam_call(sources, where, arrays, so_far=()):
     layers, d, ff = arrays[0].shape
-    row = pl.BlockSpec((1, LANES, ff), lambda l, r, s: (l, r, 0))
-    column = pl.BlockSpec((1, ff, LANES), lambda l, r, s: (l, 0, r))
+    sources = [source if isinstance(source, tuple) else (source,) for source in sources]
+    row = pl.BlockSpec((1, LANES, ff), lambda s, where: (where[s, 0], where[s, 1], 0))
+    column = pl.BlockSpec((1, ff, LANES), lambda s, where: (where[s, 0], 0, where[s, 1]))
     specs = [row, row, column] * 3
+    flat, g_specs, steps, start = [], [], [], 0
+    for source in sources:
+        size = LANES // len(source)
+        blocks = source[0].shape[0] // size
+        for array in source:
+            flat.append(array)
+            g_specs.append(pl.BlockSpec((size, 3 * ff), lambda s, where, start=start, blocks=blocks: (jnp.clip(s - start, 0, blocks - 1), 0)))
+        steps.append((blocks, len(source)))
+        start += blocks
+    elements = start * 3 * LANES * ff
     return pl.pallas_call(
-        adam_kernel,
+        functools.partial(adam_kernel, steps),
         grid_spec=pltpu.PrefetchScalarGridSpec(
             num_scalar_prefetch=1,
-            grid=(layers, d // LANES),
-            in_specs=[pl.BlockSpec((1, LANES, 3 * ff), lambda l, r, s: (l, r, 0))] + specs,
+            grid=(start,),
+            in_specs=g_specs + specs + [pl.BlockSpec(memory_space=pl.ANY)] * len(so_far),
             out_specs=specs,
         ),
         out_shape=[jax.ShapeDtypeStruct(a.shape, a.dtype) for a in arrays],
+        input_output_aliases={1 + len(flat) + 9 + i: i for i in range(len(so_far))},
         compiler_params=pltpu.CompilerParams(vmem_limit_bytes=60_000_000),
+        cost_estimate=pl.CostEstimate(flops=600 * elements, bytes_accessed=22 * elements, transcendentals=elements),
         name="adam",
-    )(jnp.zeros((1,), jnp.int32), g, *arrays)
+    )(where, *flat, *arrays, *so_far)
 
 
 def solution(mesh):
+    n = mesh.shape["dp"]
+    ahead = [(i, (i + 1) % n) for i in range(n)]
+    back = [(i, (i - 1) % n) for i in range(n)]
+
     def step(x, dy, *arrays):
-        g = main_call(x, dy, *arrays[:3])
-        g = lax.psum(g, "dp")
-        return tuple(adam_call(g, arrays))
+        me = lax.axis_index("dp")
+
+        def where(layer, *owners):
+            return jnp.stack([jnp.stack([jnp.int32(layer), lax.rem(me + i, n).astype(jnp.int32)]) for i in owners])
+
+        summed, own = main_call(n, x, dy, *arrays[:3])
+        half = own.shape[0] // 2
+        from_left, from_right = lax.ppermute(own, "dp", ahead), lax.ppermute(own, "dp", back)
+        everyone = jnp.concatenate([jnp.array([[1, i] for i in range(n)], jnp.int32), where(0, 0)])
+        new = adam_call([summed, own], everyone, arrays)
+        from_left, from_right, *new = lax.optimization_barrier((from_left, from_right, *new))
+        top, bottom = lax.ppermute(from_left[:half], "dp", ahead), lax.ppermute(from_right[half:], "dp", back)
+        new = adam_call([from_left, from_right], where(0, n - 1, 1), arrays, new)
+        return tuple(adam_call([(top, bottom)], where(0, 2), arrays, new))
 
     return jax.shard_map(
         step,

time: 403 us -> 254 us (0.63)
  waiting for transfers between devices: 185 us -> 0.01 us
  Pallas kernels: 204 us -> 243 us
  between operations: 14.1 us -> 0.9 us
  starting transfers between devices: 0.06 us -> 5.34 us
    psum x1 -> x0, waiting for transfers between devices: 184 us -> none  [step(): g = lax.psum(g, 'dp')]
    pallas_call x2 -> x4, Pallas kernels: 204 us -> 243 us  [the longest x1 197 us: main_call(): pl.pallas_call(functools.partial(main_kernel, n), out_shape=[jax.ShapeDty...]
    ppermute x0 -> x4, starting transfers between devices: none -> 5.34 us  [the longest x1 3.23 us: step(): lax.ppermute(from_right[half:], 'dp', back)]
  transfers between devices with their start and end apart: 1 -> 4, of which waited for: 1 -> 0; matrix products, arithmetic and copies ran while one was open for 0% -> 1% of each run, Pallas kernels for 0% -> 15%
where the time goes in v2:
time: 254 us
  Pallas kernels  243 us (96%)
  starting transfers between devices  5.34 us (2%)
  local copies, waits for them, and re-layouts  2.72 us (1%)
    pallas_call x1, Pallas kernels, main_call(): pl.pallas_call(functools.partial(main_kernel, n), out_shape=[jax.ShapeDty...  197 us
    pallas_call x3, Pallas kernels, adam_call(): pl.pallas_call(functools.partial(adam_kernel, steps), grid_spec=pltpu.Pre...  46 us
  transfers between devices with their start and end apart: 4, of which 0 were waited for; matrix products, arithmetic and copies ran while one was open for 1% of the time, Pallas kernels for 15%

profile of v2, /device:TPU:112, one launch (start us, length us, event | category | flops | bytes accessed | tf_op | source)
XLA Modules:
  0.0 254.1 jit_solution(12672009369022045084)
XLA Ops:
  0.6 0.0 copy-start.3
  0.7 197.2 %main.1 = (bf16[512,4992]{1,0:T(8,128)(2,1)}, bf16[128,4992]{1,0:T(8,128)(2,1)}) custom-call(bf16[1,4096,512]{2,1,0:T(8,128)(2,1)} %x_hbm.1, bf16[1,4096,512]{2,1,0:T(8,128)(2,1)} %dy_hbm.1, bf16[2,512,1664]{2,1,0:T(8,128)(2,1)} %refs_2_.5, bf16[2,512,1664]{2,1,0:T(8,128)(2,1)} %refs_3_.5, bf16[2,1664,512]{2,1,0:T(8,128)(2,1)} %refs_4_.5), custom_call_target="tpu_custom_call" | custom-call | tf_op jit(solution)/shard_map/main/pallas_call | solution.py:294
  197.8 0.7 collective-permute-start.1
  198.5 1.4 collective-permute-start
  199.9 0.1 fusion.1
  200.0 0.0 copy-done.3
  200.0 0.6 pad_add_fusion.where
  200.6 27.7 %adam.3 = (bf16[2,512,1664]{2,1,0:T(8,128)(2,1)}, bf16[2,512,1664]{2,1,0:T(8,128)(2,1)}, bf16[2,1664,512]{2,1,0:T(8,128)(2,1)}, f32[2,512,1664]{2,1,0:T(8,128)},...) custom-call(s32[5,2]{1,0:T(8,128)} %pad_add_fusion.where, ...), custom_call_target="tpu_custom_call" | custom-call | flops 1916928000 | bytes 70287360 | tf_op jit(solution)/shard_map/adam/pallas_call | solution.py:373
  228.3 0.0 collective-permute-done.1.refs_1_
  228.3 0.0 copy-start
  228.4 0.0 collective-permute-done.refs_0_
  228.4 0.0 copy-start.1
  228.4 1.0 slice.7
  229.4 0.9 slice.6
  230.3 0.0 collective-permute-start.2
  230.3 3.2 %collective-permute-start.3 = (bf16[64,4992]{1,0:T(8,128)(2,1)}, bf16[64,4992]{1,0:T(8,128)(2,1)}, u32[]{:S(2)}, u32[]{:S(2)}) collective-permute-start(bf16[64,4992]{1,0:T(8,128)(2,1)} %slice.7), channel_id=1, source_target_pairs={{0,3},{1,0},{2,1},{3,2},{4,7},{5,4},{6,5},{7,6},{8,11},{9,8},{10,9... | collective-permute-start | bytes 1916936 | tf_op jit(solution)/shard_map/ppermute | solution.py:406
  233.5 0.7 fusion.where
  234.1 0.1 fusion.2
  234.2 0.6 pad_add_fusion.1.where
  234.8 0.0 copy-done
  234.8 0.0 copy-done.1
  234.8 11.0 %adam.4 = (bf16[2,512,1664]{2,1,0:T(8,128)(2,1)}, bf16[2,512,1664]{2,1,0:T(8,128)(2,1)}, bf16[2,1664,512]{2,1,0:T(8,128)(2,1)}, f32[2,512,1664]{2,1,0:T(8,128)},...) custom-call(s32[2,2]{1,0:T(2,128)} %pad_add_fusion.1.where, ...), custom_call_target="tpu_custom_call", output_to_operand_aliasing={{0}: (12, {}), {1}: (13, {}), {2}: (14, {}), {3}: (15, {}),... | custom-call | flops 766771200 | bytes 28114944 | tf_op jit(solution)/shard_map/adam/pallas_call | solution.py:373
  245.8 0.0 collective-permute-done.2.refs_0_
  245.8 0.0 copy-start.2
  245.8 0.0 collective-permute-done.3.refs_1_
  245.8 0.8 copy-done.2
  246.7 7.3 %adam.5 = (bf16[2,512,1664]{2,1,0:T(8,128)(2,1)}, bf16[2,512,1664]{2,1,0:T(8,128)(2,1)}, bf16[2,1664,512]{2,1,0:T(8,128)(2,1)}, f32[2,512,1664]{2,1,0:T(8,128)},...) custom-call(s32[1,2]{1,0:T(1,128)} %fusion.where, ...), custom_call_target="tpu_custom_call", output_to_operand_aliasing={{0}: (12, {}), {1}: (13, {}), {2}: (14, {}), {3}: (15, {}),... | custom-call | flops 383385600 | bytes 14057472 | tf_op jit(solution)/shard_map/adam/pallas_call | solution.py:373
Async XLA Ops:
  0.6 199.4 %copy-start.3 = (s32[4,2]{1,0:T(4,128)S(1)}, s32[4,2]{1,0:T(4,128)}, u32[]{:S(2)}) copy-start(s32[4,2]{1,0:T(4,128)} %constant.24.clone) | copy-start | bytes 100
  197.8 30.5 %collective-permute-start.1 = (bf16[128,4992]{1,0:T(8,128)(2,1)}, bf16[128,4992]{1,0:T(8,128)(2,1)S(1)}, u32[]{:S(2)}, u32[]{:S(2)}) collective-permute-start(bf16[128,4992]{1,0:T(8,128)(2,1)} %get-tuple-element.40.refs_1_), channel_id=1, source_target_pairs={{0,3},{1,0},{2,1},{3,2},{4,7},{5,4},{6,5},{7,6},{8,11},{9,8},{10,9... | collective-permute-start | bytes 3833864 | tf_op jit(solution)/shard_map/ppermute | solution.py:402
  198.5 29.9 %collective-permute-start = (bf16[128,4992]{1,0:T(8,128)(2,1)}, bf16[128,4992]{1,0:T(8,128)(2,1)S(1)}, u32[]{:S(2)}, u32[]{:S(2)}) collective-permute-start(bf16[128,4992]{1,0:T(8,128)(2,1)} %get-tuple-element.40.refs_1_), channel_id=1, source_target_pairs={{0,1},{1,2},{2,3},{3,0},{4,5},{5,6},{6,7},{7,4},{8,9},{9,10},{10,1... | collective-permute-start | bytes 3833864 | tf_op jit(solution)/shard_map/ppermute | solution.py:402
  228.3 6.5 %copy-start = (bf16[128,4992]{1,0:T(8,128)(2,1)}, bf16[128,4992]{1,0:T(8,128)(2,1)S(1)}, u32[]{:S(2)}) copy-start(bf16[128,4992]{1,0:T(8,128)(2,1)S(1)} %collective-permute-done.1.refs_1_) | copy-start | bytes 3833860
  228.4 6.5 %copy-start.1 = (bf16[128,4992]{1,0:T(8,128)(2,1)}, bf16[128,4992]{1,0:T(8,128)(2,1)S(1)}, u32[]{:S(2)}) copy-start(bf16[128,4992]{1,0:T(8,128)(2,1)S(1)} %collective-permute-done.refs_0_) | copy-start | bytes 3833860
  230.3 15.6 %collective-permute-start.2 = (bf16[64,4992]{1,0:T(8,128)(2,1)}, bf16[64,4992]{1,0:T(8,128)(2,1)S(1)}, u32[]{:S(2)}, u32[]{:S(2)}) collective-permute-start(bf16[64,4992]{1,0:T(8,128)(2,1)} %slice.6), channel_id=1, source_target_pairs={{0,1},{1,2},{2,3},{3,0},{4,5},{5,6},{6,7},{7,4},{8,9},{9,10},{10,1... | collective-permute-start | bytes 1916936 | tf_op jit(solution)/shard_map/ppermute | solution.py:406
  230.3 15.6 %collective-permute-start.3 = (bf16[64,4992]{1,0:T(8,128)(2,1)}, bf16[64,4992]{1,0:T(8,128)(2,1)}, u32[]{:S(2)}, u32[]{:S(2)}) collective-permute-start(bf16[64,4992]{1,0:T(8,128)(2,1)} %slice.7), channel_id=1, source_target_pairs={{0,3},{1,0},{2,1},{3,2},{4,7},{5,4},{6,5},{7,6},{8,11},{9,8},{10,9... | collective-permute-start | bytes 1916936 | tf_op jit(solution)/shard_map/ppermute | solution.py:406
  245.8 0.8 copy-start.2

commit v3 on v2

--- a/solution.py
+++ b/solution.py
@@ -11,6 +11,7 @@
 WIDE = 256
 LANES = 128
 TILE = 1024
+FORWARD = 1024
 ROWS = 512
 
 
@@ -130,12 +131,6 @@
         else:
             pl.when(condition)(lambda: action(*args))
 
-    def meanwhile(layer, k):
-        when(k >= 2, finish, layer, k - 2)
-        when(k >= 1, start_two, layer, k - 1)
-        if not layer:
-            start_far(k)
-
     def weight_copies(layer):
         copies = []
         for k, width in enumerate(widths):
@@ -161,8 +156,9 @@
         copy.wait()
 
     def forward(t, carry):
-        rows = at(t, ROWS)
-        x_copy(t, h_ref).wait()
+        rows = at(t, FORWARD)
+        for i in range(FORWARD // ROWS):
+            x_copy(t * (FORWARD // ROWS) + i, h_ref).wait()
         x = h_ref[rows, :]
         a = normed(x)
         for k, width in enumerate(widths):
@@ -176,7 +172,7 @@
         at_ref[:, rows] = a.T
         return carry
 
-    lax.fori_loop(0, steps, forward, 0)
+    lax.fori_loop(0, tokens // FORWARD, forward, 0)
     dy_copy.wait()
 
     def turn(t, carry):
@@ -189,7 +185,7 @@
         for copy in weight_copies(layer):
             copy.wait()
 
-    def chunk(layer, k, width, first, last):
+    def chunk(layer, k, width, first):
         gu_cols = pl.ds(pl.multiple_of(k * 2 * WIDE, 2 * WIDE), 2 * width)
         down_rows = pl.ds(pl.multiple_of(k * WIDE, WIDE), width)
 
@@ -206,7 +202,16 @@
             return carry
 
         lax.fori_loop(0, tokens // TILE, hidden, 0)
-        meanwhile(layer, k)
+        if layer:
+
+            @pl.when(k == full - 1)
+            def _():
+                for t in range(steps):
+                    x_copy(t, a_ref).start()
+
+        else:
+            when(k >= 3, finish, layer, k - 3)
+            when(k + 3 < full, start_far, k + 3)
         dgu = dot(at_ref[...], dgu_ref[:, pl.ds(0, 2 * width)]).astype(BF16)
         down = dot(gt_ref[...], hid_ref[:, pl.ds(0, width)]).astype(BF16)
         for j in range(width // LANES):
@@ -214,45 +219,30 @@
                 term_ref[:, pl.ds(pl.multiple_of(k * 3 * WIDE, 3 * WIDE) + (3 * j + i) * LANES, LANES)] = piece
         start_one(layer, k)
         if layer:
+            when(k == 0, start_two, layer, last)
+            when((k >= 1) & (k < full), start_two, layer, k - 1)
+        else:
+            when(k >= 1, start_two, layer, k - 1)
+        if layer:
 
             def by_a(t, carry):
                 rows = at(t, TILE)
                 part = dot_t(dgu_ref[rows, pl.ds(0, 2 * width)], wgu_ref[layer, :, gu_cols])
-                if first is True:
+                if first:
                     da_ref[rows, :] = part
                 else:
                     da_ref[rows, :] += part
                 return carry
 
             lax.fori_loop(0, tokens // TILE, by_a, 0)
-
-    def backward(layer):
-        if layer:
-            chunk(layer, 0, WIDE, True, False)
-
-            def body(k, carry):
-                chunk(layer, k, WIDE, False, False)
-                return carry
-
-            lax.fori_loop(1, full, body, 0)
-        else:
-
-            def body(k, carry):
-                chunk(layer, k, WIDE, False, False)
-                return carry
-
-            lax.fori_loop(0, full, body, 0)
-        for k in range(full, len(widths)):
-            chunk(layer, k, widths[k], False, True)
+            when(k == 1, finish, layer, last)
+            when((k >= 2) & (k < full), finish, layer, k - 2)
 
     last = len(widths) - 1
     pl.semaphore_wait(barrier, 2)
-    backward(1)
-    finish(1, last - 1)
-    start_two(1, last)
-
-    for t in range(steps):
-        x_copy(t, a_ref).start()
+    chunk(1, last, widths[last], True)
+    lax.fori_loop(0, full, lambda k, carry: (chunk(1, k, WIDE, False), carry)[1], 0)
+
 
     def between(t, carry):
         rows = at(t, ROWS)
@@ -270,11 +260,20 @@
         at_ref[:, rows] = a.T
         return carry
 
-    lax.fori_loop(0, steps, between, 0)
-    finish(1, last)
-    backward(0)
+    lax.fori_loop(0, steps // 2, between, 0)
+    start_two(1, full - 1)
+    finish(1, full - 2)
+    start_far(last)
+    start_far(0)
+    lax.fori_loop(steps // 2, steps, between, 0)
+    finish(1, full - 1)
+    start_far(1)
+    start_far(2)
+    lax.fori_loop(0, full, lambda k, carry: (chunk(0, k, WIDE, False), carry)[1], 0)
+    chunk(0, last, widths[last], False)
+    finish(0, last - 2)
+    start_two(0, last)
     finish(0, last - 1)
-    start_two(0, last)
     finish(0, last)
     for k in range(len(widths)):
         keep(0, k).wait()
@@ -305,7 +304,7 @@
             pltpu.VMEM((tokens, d), F32),
             pltpu.VMEM((layers, d, 2 * ff), BF16),
             pltpu.VMEM((layers, ff, d), BF16),
-            pltpu.VMEM((ROWS, ff), BF16),
+            pltpu.VMEM((FORWARD, ff), BF16),
             pltpu.VMEM((tokens, WIDE), BF16),
             pltpu.VMEM((tokens, 2 * WIDE), BF16),
             pltpu.VMEM((d, 3 * ff), BF16),
@@ -330,17 +329,17 @@
     return (w - 0.02 * step).astype(BF16), m, v
 
 
-def adam_kernel(sources, where, *refs):
+def adam_kernel(sources, me, *refs):
     count = sum(parts for _, parts in sources)
     ins, outs = refs[count : count + 9], refs[-9:]
-    ff = ins[0].shape[-1]
+    units = ins[0].shape[-1]
     start = 0
     for steps, parts in sources:
         mine, refs = refs[:parts], refs[parts:]
 
         @pl.when((pl.program_id(0) >= start) & (pl.program_id(0) < start + steps))
         def _(mine=mine):
-            for j in range(ff // LANES):
+            for j in range(units // LANES):
                 cols = pl.ds(j * LANES, LANES)
                 for i in range(3):
                     g = [ref[:, pl.ds((3 * j + i) * LANES, LANES)].astype(F32) for ref in mine]
@@ -354,11 +353,19 @@
         start += steps
 
 
-def adam_call(sources, where, arrays, so_far=()):
+def adam_call(me, places, sources, arrays, so_far=()):
     layers, d, ff = arrays[0].shape
     sources = [source if isinstance(source, tuple) else (source,) for source in sources]
-    row = pl.BlockSpec((1, LANES, ff), lambda s, where: (where[s, 0], where[s, 1], 0))
-    column = pl.BlockSpec((1, ff, LANES), lambda s, where: (where[s, 0], 0, where[s, 1]))
+
+    def at_row(s, me):
+        layer, place = places(s, me[0])
+        return layer, place, 0
+
+    def at_column(s, me):
+        layer, place = places(s, me[0])
+        return layer, 0, place
+
+    row, column = pl.BlockSpec((1, LANES, ff), at_row), pl.BlockSpec((1, ff, LANES), at_column)
     specs = [row, row, column] * 3
     flat, g_specs, steps, start = [], [], [], 0
     for source in sources:
@@ -366,7 +373,7 @@
         blocks = source[0].shape[0] // size
         for array in source:
             flat.append(array)
-            g_specs.append(pl.BlockSpec((size, 3 * ff), lambda s, where, start=start, blocks=blocks: (jnp.clip(s - start, 0, blocks - 1), 0)))
+            g_specs.append(pl.BlockSpec((size, 3 * ff), lambda s, me, start=start, blocks=blocks: (jnp.clip(s - start, 0, blocks - 1), 0)))
         steps.append((blocks, len(source)))
         start += blocks
     elements = start * 3 * LANES * ff
@@ -383,7 +390,7 @@
         compiler_params=pltpu.CompilerParams(vmem_limit_bytes=60_000_000),
         cost_estimate=pl.CostEstimate(flops=600 * elements, bytes_accessed=22 * elements, transcendentals=elements),
         name="adam",
-    )(where, *flat, *arrays, *so_far)
+    )(me, *flat, *arrays, *so_far)
 
 
 def solution(mesh):
@@ -392,20 +399,23 @@
     back = [(i, (i - 1) % n) for i in range(n)]
 
     def step(x, dy, *arrays):
-        me = lax.axis_index("dp")
-
-        def where(layer, *owners):
-            return jnp.stack([jnp.stack([jnp.int32(layer), lax.rem(me + i, n).astype(jnp.int32)]) for i in owners])
-
+        me = lax.axis_index("dp").astype(jnp.int32)[None]
+
+        def place(*steps):
+            return lambda s, me: (0, lax.rem(me + steps[0] + s * (steps[-1] - steps[0]), n))
+
+        def everyone(s, me):
+            return jnp.where(s < n, 1, 0), jnp.where(s < n, s, me)
+
+        x, me = lax.optimization_barrier((x, me))
         summed, own = main_call(n, x, dy, *arrays[:3])
         half = own.shape[0] // 2
         from_left, from_right = lax.ppermute(own, "dp", ahead), lax.ppermute(own, "dp", back)
-        everyone = jnp.concatenate([jnp.array([[1, i] for i in range(n)], jnp.int32), where(0, 0)])
-        new = adam_call([summed, own], everyone, arrays)
+        new = adam_call(me, everyone, [summed, own], arrays)
         from_left, from_right, *new = lax.optimization_barrier((from_left, from_right, *new))
         top, bottom = lax.ppermute(from_left[:half], "dp", ahead), lax.ppermute(from_right[half:], "dp", back)
-        new = adam_call([from_left, from_right], where(0, n - 1, 1), arrays, new)
-        return tuple(adam_call([(top, bottom)], where(0, 2), arrays, new))
+        new = adam_call(me, place(n - 1, n + 1), [from_left, from_right], arrays, new)
+        return tuple(adam_call(me, place(2), [(top, bottom)], arrays, new))
 
     return jax.shard_map(
         step,

time: 254 us -> 244 us (0.961)
  Pallas kernels: 243 us -> 231 us
  waiting for transfers between devices: 0.01 us -> 4.55 us
    pallas_call x1, Pallas kernels: 197 us -> 188 us  [main_call(): pl.pallas_call(functools.partial(main_kernel, n), out_shape=[jax.ShapeDty...]
    ppermute x1, waiting for transfers between devices: 0.01 us -> 2.76 us  [step(): lax.ppermute(own, 'dp', ahead)]
  transfers between devices with their start and end apart: 4 -> 4, of which waited for: 0 -> 2; matrix products, arithmetic and copies ran while one was open for 1% -> 0% of each run, Pallas kernels for 15% -> 15%
where the time goes in v3:
time: 244 us
  Pallas kernels  231 us (95%)
  starting transfers between devices  5.85 us (2%)
  waiting for transfers between devices  4.55 us (2%)
    pallas_call x1, Pallas kernels, main_call(): pl.pallas_call(functools.partial(main_kernel, n), out_shape=[jax.ShapeDty...  188 us
    pallas_call x3, Pallas kernels, adam_call(): pl.pallas_call(functools.partial(adam_kernel, steps), grid_spec=pltpu.Pre...  43.8 us
  transfers between devices with their start and end apart: 4, of which 2 were waited for; matrix products, arithmetic and copies ran while one was open for 0% of the time, Pallas kernels for 15%

profile of v3, /device:TPU:112, one launch (start us, length us, event | category | flops | bytes accessed | tf_op | source)
XLA Modules:
  0.0 243.8 jit_solution(7671433905347984575)
XLA Ops:
  0.6 187.6 %main.1 = (bf16[512,4992]{1,0:T(8,128)(2,1)}, bf16[128,4992]{1,0:T(8,128)(2,1)}) custom-call(bf16[1,4096,512]{2,1,0:T(8,128)(2,1)} %x_hbm, bf16[1,4096,512]{2,1,0:T(8,128)(2,1)} %dy_hbm.1, bf16[2,512,1664]{2,1,0:T(8,128)(2,1)} %refs_2_.5, bf16[2,512,1664]{2,1,0:T(8,128)(2,1)} %refs_3_.5, bf16[2,1664,512]{2,1,0:T(8,128)(2,1)} %refs_4_.5), custom_call_target="tpu_custom_call" | custom-call | tf_op jit(solution)/shard_map/main/pallas_call | solution.py:293
  188.3 2.5 %collective-permute-start.1 = (bf16[128,4992]{1,0:T(8,128)(2,1)}, bf16[128,4992]{1,0:T(8,128)(2,1)S(1)}, u32[]{:S(2)}, u32[]{:S(2)}) collective-permute-start(bf16[128,4992]{1,0:T(8,128)(2,1)} %get-tuple-element.44.refs_1_), channel_id=1, source_target_pairs={{0,3},{1,0},{2,1},{3,2},{4,7},{5,4},{6,5},{7,6},{8,11},{9,8},{10,9... | collective-permute-start | bytes 3833864 | tf_op jit(solution)/shard_map/ppermute | solution.py:413
  190.8 0.0 collective-permute-start
  190.8 27.0 %adam.3 = (bf16[2,512,1664]{2,1,0:T(8,128)(2,1)}, bf16[2,512,1664]{2,1,0:T(8,128)(2,1)}, bf16[2,1664,512]{2,1,0:T(8,128)(2,1)}, f32[2,512,1664]{2,1,0:T(8,128)},...) custom-call(s32[1]{0:T(128)} %bitcast.me, ...), custom_call_target="tpu_custom_call" | custom-call | flops 1916928000 | bytes 70287360 | tf_op jit(solution)/shard_map/adam/pallas_call | solution.py:380
  217.8 0.0 collective-permute-done.1.refs_1_
  217.8 0.0 copy-start
  217.8 2.8 %collective-permute-done.refs_0_ = bf16[128,4992]{1,0:T(8,128)(2,1)S(1)} collective-permute-done((bf16[128,4992]{1,0:T(8,128)(2,1)}, bf16[128,4992]{1,0:T(8,128)(2,1)S(1)}, u32[]{:S(2)}, u32[]{:S(2)}) %collective-permute-start) | collective-permute-done | bytes 1277984 | tf_op jit(solution)/shard_map/ppermute | solution.py:413
  220.6 0.0 copy-start.1
  220.7 0.1 collective-permute-start.2
  220.8 3.2 %collective-permute-start.3 = (bf16[64,4992]{1,0:T(8,128)(2,1)S(1)}, bf16[64,4992]{1,0:T(8,128)(2,1)S(1)}, u32[]{:S(2)}, u32[]{:S(2)}) collective-permute-start(bf16[64,4992]{1,0:T(8,128)(2,1)S(1)} %slice.7), channel_id=1, source_target_pairs={{0,3},{1,0},{2,1},{3,2},{4,7},{5,4},{6,5},{7,6},{8,11},{9,8},{10,9... | collective-permute-start | bytes 1916936 | tf_op jit(solution)/shard_map/ppermute | solution.py:416
  224.0 0.0 copy-done
  224.0 0.0 copy-done.1
  224.0 10.2 %adam.4 = (bf16[2,512,1664]{2,1,0:T(8,128)(2,1)}, bf16[2,512,1664]{2,1,0:T(8,128)(2,1)}, bf16[2,1664,512]{2,1,0:T(8,128)(2,1)}, f32[2,512,1664]{2,1,0:T(8,128)},...) custom-call(s32[1]{0:T(128)} %bitcast.me, ...), custom_call_target="tpu_custom_call", output_to_operand_aliasing={{0}: (12, {}), {1}: (13, {}), {2}: (14, {}), {3}: (15, {}),... | custom-call | flops 766771200 | bytes 28114944 | tf_op jit(solution)/shard_map/adam/pallas_call | solution.py:380
  234.2 1.8 collective-permute-done.2.refs_0_
  236.0 0.0 copy-start.2
  236.0 0.0 collective-permute-done.3.refs_1_
  236.0 0.0 copy-start.3
  236.0 0.8 copy-done.2
  236.9 0.2 copy-done.3
  237.1 6.6 %adam.5 = (bf16[2,512,1664]{2,1,0:T(8,128)(2,1)}, bf16[2,512,1664]{2,1,0:T(8,128)(2,1)}, bf16[2,1664,512]{2,1,0:T(8,128)(2,1)}, f32[2,512,1664]{2,1,0:T(8,128)},...) custom-call(s32[1]{0:T(128)} %bitcast.me, ...), custom_call_target="tpu_custom_call", output_to_operand_aliasing={{0}: (12, {}), {1}: (13, {}), {2}: (14, {}), {3}: (15, {}),... | custom-call | flops 383385600 | bytes 14057472 | tf_op jit(solution)/shard_map/adam/pallas_call | solution.py:380
  (2 shorter events, 0.1 us)
Async XLA Ops:
  188.3 29.5 %collective-permute-start.1 = (bf16[128,4992]{1,0:T(8,128)(2,1)}, bf16[128,4992]{1,0:T(8,128)(2,1)S(1)}, u32[]{:S(2)}, u32[]{:S(2)}) collective-permute-start(bf16[128,4992]{1,0:T(8,128)(2,1)} %get-tuple-element.44.refs_1_), channel_id=1, source_target_pairs={{0,3},{1,0},{2,1},{3,2},{4,7},{5,4},{6,5},{7,6},{8,11},{9,8},{10,9... | collective-permute-start | bytes 3833864 | tf_op jit(solution)/shard_map/ppermute | solution.py:413
  190.8 29.8 %collective-permute-start = (bf16[128,4992]{1,0:T(8,128)(2,1)}, bf16[128,4992]{1,0:T(8,128)(2,1)S(1)}, u32[]{:S(2)}, u32[]{:S(2)}) collective-permute-start(bf16[128,4992]{1,0:T(8,128)(2,1)} %get-tuple-element.44.refs_1_), channel_id=1, source_target_pairs={{0,1},{1,2},{2,3},{3,0},{4,5},{5,6},{6,7},{7,4},{8,9},{9,10},{10,1... | collective-permute-start | bytes 3833864 | tf_op jit(solution)/shard_map/ppermute | solution.py:413
  217.8 6.2 %copy-start = (bf16[128,4992]{1,0:T(8,128)(2,1)}, bf16[128,4992]{1,0:T(8,128)(2,1)S(1)}, u32[]{:S(2)}) copy-start(bf16[128,4992]{1,0:T(8,128)(2,1)S(1)} %collective-permute-done.1.refs_1_) | copy-start | bytes 3833860
  220.6 3.4 %copy-start.1 = (bf16[128,4992]{1,0:T(8,128)(2,1)}, bf16[128,4992]{1,0:T(8,128)(2,1)S(1)}, u32[]{:S(2)}) copy-start(bf16[128,4992]{1,0:T(8,128)(2,1)S(1)} %collective-permute-done.refs_0_) | copy-start | bytes 3833860
  220.7 15.3 %collective-permute-start.2 = (bf16[64,4992]{1,0:T(8,128)(2,1)S(1)}, bf16[64,4992]{1,0:T(8,128)(2,1)S(1)}, u32[]{:S(2)}, u32[]{:S(2)}) collective-permute-start(bf16[64,4992]{1,0:T(8,128)(2,1)S(1)} %slice.6), channel_id=1, source_target_pairs={{0,1},{1,2},{2,3},{3,0},{4,5},{5,6},{6,7},{7,4},{8,9},{9,10},{10,1... | collective-permute-start | bytes 1916936 | tf_op jit(solution)/shard_map/ppermute | solution.py:416
  220.8 15.2 %collective-permute-start.3 = (bf16[64,4992]{1,0:T(8,128)(2,1)S(1)}, bf16[64,4992]{1,0:T(8,128)(2,1)S(1)}, u32[]{:S(2)}, u32[]{:S(2)}) collective-permute-start(bf16[64,4992]{1,0:T(8,128)(2,1)S(1)} %slice.7), channel_id=1, source_target_pairs={{0,3},{1,0},{2,1},{3,2},{4,7},{5,4},{6,5},{7,6},{8,11},{9,8},{10,9... | collective-permute-start | bytes 1916936 | tf_op jit(solution)/shard_map/ppermute | solution.py:416
  236.0 0.8 copy-start.2
  236.0 1.1 copy-start.3

commit v4 on v3

--- a/solution.py
+++ b/solution.py
@@ -41,7 +41,7 @@
 def main_kernel(
     n, x_hbm, dy_hbm, wg_hbm, wu_hbm, wd_hbm,
     all_hbm, own_hbm,
-    h_ref, a_ref, at_ref, g_ref, gt_ref, da_ref, wgu_ref, wd_ref, mid_ref, hid_ref, dgu_ref, term_ref, one_ref, two_ref,
+    h_ref, a_ref, at_ref, g_ref, gt_ref, da_ref, wgu_ref, wd_ref, hid_ref, dgu_ref, term_ref, one_ref, two_ref,
     w_sem, x_sem, dy_sem, one_send, one_recv, two_send, two_recv, near_send, near_recv, far_send, far_recv, keep_sem,
 ):
     tokens, d = h_ref.shape
@@ -164,8 +164,12 @@
         for k, width in enumerate(widths):
             gu = dot(a, wgu_ref[0, :, pl.ds(2 * k * WIDE, 2 * width)])
             gate, up = gu[:, :width], gu[:, width:]
-            mid_ref[:, pl.ds(k * WIDE, width)] = (gate * jax.nn.sigmoid(gate) * up).astype(BF16)
-        h = (x.astype(F32) + dot(mid_ref[...], wd_ref[0]).astype(BF16).astype(F32)).astype(BF16)
+            dgu_ref[pl.ds(k // 2 * FORWARD, FORWARD), pl.ds(k % 2 * WIDE, width)] = (gate * jax.nn.sigmoid(gate) * up).astype(BF16)
+        down = 0.0
+        for k in range(0, len(widths), 2):
+            width = sum(widths[k : k + 2])
+            down += dot(dgu_ref[pl.ds(k // 2 * FORWARD, FORWARD), pl.ds(0, width)], wd_ref[0, pl.ds(k * WIDE, width), :])
+        h = (x.astype(F32) + down.astype(BF16).astype(F32)).astype(BF16)
         h_ref[rows, :] = h
         a = normed(h)
         a_ref[rows, :] = a
@@ -190,7 +194,7 @@
         down_rows = pl.ds(pl.multiple_of(k * WIDE, WIDE), width)
 
         def hidden(t, carry):
-            rows = at(t, TILE)
+            rows = at(t, 2 * TILE)
             gu = dot(a_ref[rows, :], wgu_ref[layer, :, gu_cols])
             dh = dot_t(g_ref[rows, :], wd_ref[layer, down_rows, :]).astype(BF16).astype(F32)
             gate, up = gu[:, :width], gu[:, width:]
@@ -201,8 +205,10 @@
             dgu_ref[rows, pl.ds(0, width)] = (dh * up * (s + silu * (1.0 - s))).astype(BF16)
             return carry
 
-        lax.fori_loop(0, tokens // TILE, hidden, 0)
+        lax.fori_loop(0, tokens // (2 * TILE), hidden, 0)
         if layer:
+            when(k == 0, start_two, layer, last)
+            when((k >= 1) & (k < full), start_two, layer, k - 1)
 
             @pl.when(k == full - 1)
             def _():
@@ -218,10 +224,7 @@
             for i, piece in enumerate((dgu[:, j * LANES : (j + 1) * LANES], dgu[:, width + j * LANES : width + (j + 1) * LANES], down[:, j * LANES : (j + 1) * LANES])):
                 term_ref[:, pl.ds(pl.multiple_of(k * 3 * WIDE, 3 * WIDE) + (3 * j + i) * LANES, LANES)] = piece
         start_one(layer, k)
-        if layer:
-            when(k == 0, start_two, layer, last)
-            when((k >= 1) & (k < full), start_two, layer, k - 1)
-        else:
+        if not layer:
             when(k >= 1, start_two, layer, k - 1)
         if layer:
 
@@ -235,7 +238,7 @@
                 return carry
 
             lax.fori_loop(0, tokens // TILE, by_a, 0)
-            when(k == 1, finish, layer, last)
+            when(k == 0, finish, layer, last)
             when((k >= 2) & (k < full), finish, layer, k - 2)
 
     last = len(widths) - 1
@@ -260,12 +263,12 @@
         at_ref[:, rows] = a.T
         return carry
 
-    lax.fori_loop(0, steps // 2, between, 0)
+    lax.fori_loop(0, steps // 4, between, 0)
     start_two(1, full - 1)
     finish(1, full - 2)
     start_far(last)
     start_far(0)
-    lax.fori_loop(steps // 2, steps, between, 0)
+    lax.fori_loop(steps // 4, steps, between, 0)
     finish(1, full - 1)
     start_far(1)
     start_far(2)
@@ -304,7 +307,6 @@
             pltpu.VMEM((tokens, d), F32),
             pltpu.VMEM((layers, d, 2 * ff), BF16),
             pltpu.VMEM((layers, ff, d), BF16),
-            pltpu.VMEM((FORWARD, ff), BF16),
             pltpu.VMEM((tokens, WIDE), BF16),
             pltpu.VMEM((tokens, 2 * WIDE), BF16),
             pltpu.VMEM((d, 3 * ff), BF16),

time: 244 us -> 239 us (0.980)
  Pallas kernels: 231 us -> 227 us
    pallas_call x1, Pallas kernels: 188 us -> 183 us  [main_call(): pl.pallas_call(functools.partial(main_kernel, n), out_shape=[jax.ShapeDty...]
  transfers between devices with their start and end apart: 4 -> 4, of which waited for: 2 -> 2; matrix products, arithmetic and copies ran while one was open for 0% -> 0% of each run, Pallas kernels for 15% -> 16%
where the time goes in v4:
time: 239 us
  Pallas kernels  227 us (95%)
  starting transfers between devices  5.89 us (2%)
  waiting for transfers between devices  4.6 us (2%)
    pallas_call x1, Pallas kernels, main_call(): pl.pallas_call(functools.partial(main_kernel, n), out_shape=[jax.ShapeDty...  183 us
    pallas_call x3, Pallas kernels, adam_call(): pl.pallas_call(functools.partial(adam_kernel, steps), grid_spec=pltpu.Pre...  43.8 us
  transfers between devices with their start and end apart: 4, of which 2 were waited for; matrix products, arithmetic and copies ran while one was open for 0% of the time, Pallas kernels for 16%

profile of v4, /device:TPU:112, one launch (start us, length us, event | category | flops | bytes accessed | tf_op | source)
XLA Modules:
  0.0 239.2 jit_solution(9763300820527586068)
XLA Ops:
  0.6 182.8 %main.1 = (bf16[512,4992]{1,0:T(8,128)(2,1)}, bf16[128,4992]{1,0:T(8,128)(2,1)}) custom-call(bf16[1,4096,512]{2,1,0:T(8,128)(2,1)} %x_hbm, bf16[1,4096,512]{2,1,0:T(8,128)(2,1)} %dy_hbm.1, bf16[2,512,1664]{2,1,0:T(8,128)(2,1)} %refs_2_.5, bf16[2,512,1664]{2,1,0:T(8,128)(2,1)} %refs_3_.5, bf16[2,1664,512]{2,1,0:T(8,128)(2,1)} %refs_4_.5), custom_call_target="tpu_custom_call" | custom-call | tf_op jit(solution)/shard_map/main/pallas_call | solution.py:296
  183.5 2.6 %collective-permute-start.1 = (bf16[128,4992]{1,0:T(8,128)(2,1)}, bf16[128,4992]{1,0:T(8,128)(2,1)S(1)}, u32[]{:S(2)}, u32[]{:S(2)}) collective-permute-start(bf16[128,4992]{1,0:T(8,128)(2,1)} %get-tuple-element.44.refs_1_), channel_id=1, source_target_pairs={{0,3},{1,0},{2,1},{3,2},{4,7},{5,4},{6,5},{7,6},{8,11},{9,8},{10,9... | collective-permute-start | bytes 3833864 | tf_op jit(solution)/shard_map/ppermute | solution.py:415
  186.0 0.0 collective-permute-start
  186.0 27.0 %adam.3 = (bf16[2,512,1664]{2,1,0:T(8,128)(2,1)}, bf16[2,512,1664]{2,1,0:T(8,128)(2,1)}, bf16[2,1664,512]{2,1,0:T(8,128)(2,1)}, f32[2,512,1664]{2,1,0:T(8,128)},...) custom-call(s32[1]{0:T(128)} %bitcast.me, ...), custom_call_target="tpu_custom_call" | custom-call | flops 1916928000 | bytes 70287360 | tf_op jit(solution)/shard_map/adam/pallas_call | solution.py:382
  213.1 0.0 collective-permute-done.1.refs_1_
  213.1 0.0 copy-start
  213.1 2.8 %collective-permute-done.refs_0_ = bf16[128,4992]{1,0:T(8,128)(2,1)S(1)} collective-permute-done((bf16[128,4992]{1,0:T(8,128)(2,1)}, bf16[128,4992]{1,0:T(8,128)(2,1)S(1)}, u32[]{:S(2)}, u32[]{:S(2)}) %collective-permute-start) | collective-permute-done | bytes 1277984 | tf_op jit(solution)/shard_map/ppermute | solution.py:415
  215.9 0.0 copy-start.1
  216.0 0.1 collective-permute-start.2
  216.1 3.2 %collective-permute-start.3 = (bf16[64,4992]{1,0:T(8,128)(2,1)S(1)}, bf16[64,4992]{1,0:T(8,128)(2,1)S(1)}, u32[]{:S(2)}, u32[]{:S(2)}) collective-permute-start(bf16[64,4992]{1,0:T(8,128)(2,1)S(1)} %slice.7), channel_id=1, source_target_pairs={{0,3},{1,0},{2,1},{3,2},{4,7},{5,4},{6,5},{7,6},{8,11},{9,8},{10,9... | collective-permute-start | bytes 1916936 | tf_op jit(solution)/shard_map/ppermute | solution.py:418
  219.3 0.0 copy-done
  219.3 0.0 copy-done.1
  219.3 10.2 %adam.4 = (bf16[2,512,1664]{2,1,0:T(8,128)(2,1)}, bf16[2,512,1664]{2,1,0:T(8,128)(2,1)}, bf16[2,1664,512]{2,1,0:T(8,128)(2,1)}, f32[2,512,1664]{2,1,0:T(8,128)},...) custom-call(s32[1]{0:T(128)} %bitcast.me, ...), custom_call_target="tpu_custom_call", output_to_operand_aliasing={{0}: (12, {}), {1}: (13, {}), {2}: (14, {}), {3}: (15, {}),... | custom-call | flops 766771200 | bytes 28114944 | tf_op jit(solution)/shard_map/adam/pallas_call | solution.py:382
  229.5 1.8 collective-permute-done.2.refs_0_
  231.3 0.0 copy-start.2
  231.3 0.0 collective-permute-done.3.refs_1_
  231.3 0.0 copy-start.3
  231.3 0.8 copy-done.2
  232.1 0.2 copy-done.3
  232.4 6.6 %adam.5 = (bf16[2,512,1664]{2,1,0:T(8,128)(2,1)}, bf16[2,512,1664]{2,1,0:T(8,128)(2,1)}, bf16[2,1664,512]{2,1,0:T(8,128)(2,1)}, f32[2,512,1664]{2,1,0:T(8,128)},...) custom-call(s32[1]{0:T(128)} %bitcast.me, ...), custom_call_target="tpu_custom_call", output_to_operand_aliasing={{0}: (12, {}), {1}: (13, {}), {2}: (14, {}), {3}: (15, {}),... | custom-call | flops 383385600 | bytes 14057472 | tf_op jit(solution)/shard_map/adam/pallas_call | solution.py:382
  (2 shorter events, 0.1 us)
Async XLA Ops:
  183.5 29.6 %collective-permute-start.1 = (bf16[128,4992]{1,0:T(8,128)(2,1)}, bf16[128,4992]{1,0:T(8,128)(2,1)S(1)}, u32[]{:S(2)}, u32[]{:S(2)}) collective-permute-start(bf16[128,4992]{1,0:T(8,128)(2,1)} %get-tuple-element.44.refs_1_), channel_id=1, source_target_pairs={{0,3},{1,0},{2,1},{3,2},{4,7},{5,4},{6,5},{7,6},{8,11},{9,8},{10,9... | collective-permute-start | bytes 3833864 | tf_op jit(solution)/shard_map/ppermute | solution.py:415
  186.0 29.8 %collective-permute-start = (bf16[128,4992]{1,0:T(8,128)(2,1)}, bf16[128,4992]{1,0:T(8,128)(2,1)S(1)}, u32[]{:S(2)}, u32[]{:S(2)}) collective-permute-start(bf16[128,4992]{1,0:T(8,128)(2,1)} %get-tuple-element.44.refs_1_), channel_id=1, source_target_pairs={{0,1},{1,2},{2,3},{3,0},{4,5},{5,6},{6,7},{7,4},{8,9},{9,10},{10,1... | collective-permute-start | bytes 3833864 | tf_op jit(solution)/shard_map/ppermute | solution.py:415
  213.1 6.2 %copy-start = (bf16[128,4992]{1,0:T(8,128)(2,1)}, bf16[128,4992]{1,0:T(8,128)(2,1)S(1)}, u32[]{:S(2)}) copy-start(bf16[128,4992]{1,0:T(8,128)(2,1)S(1)} %collective-permute-done.1.refs_1_) | copy-start | bytes 3833860
  215.9 3.4 %copy-start.1 = (bf16[128,4992]{1,0:T(8,128)(2,1)}, bf16[128,4992]{1,0:T(8,128)(2,1)S(1)}, u32[]{:S(2)}) copy-start(bf16[128,4992]{1,0:T(8,128)(2,1)S(1)} %collective-permute-done.refs_0_) | copy-start | bytes 3833860
  216.0 15.4 %collective-permute-start.2 = (bf16[64,4992]{1,0:T(8,128)(2,1)S(1)}, bf16[64,4992]{1,0:T(8,128)(2,1)S(1)}, u32[]{:S(2)}, u32[]{:S(2)}) collective-permute-start(bf16[64,4992]{1,0:T(8,128)(2,1)S(1)} %slice.6), channel_id=1, source_target_pairs={{0,1},{1,2},{2,3},{3,0},{4,5},{5,6},{6,7},{7,4},{8,9},{9,10},{10,1... | collective-permute-start | bytes 1916936 | tf_op jit(solution)/shard_map/ppermute | solution.py:418
  216.1 15.3 %collective-permute-start.3 = (bf16[64,4992]{1,0:T(8,128)(2,1)S(1)}, bf16[64,4992]{1,0:T(8,128)(2,1)S(1)}, u32[]{:S(2)}, u32[]{:S(2)}) collective-permute-start(bf16[64,4992]{1,0:T(8,128)(2,1)S(1)} %slice.7), channel_id=1, source_target_pairs={{0,3},{1,0},{2,1},{3,2},{4,7},{5,4},{6,5},{7,6},{8,11},{9,8},{10,9... | collective-permute-start | bytes 1916936 | tf_op jit(solution)/shard_map/ppermute | solution.py:418
  231.3 0.8 copy-start.2
  231.3 1.1 copy-start.3

commit v5 on v4

--- a/solution.py
+++ b/solution.py
@@ -10,7 +10,7 @@
 BF16, F32 = jnp.bfloat16, jnp.float32
 WIDE = 256
 LANES = 128
-TILE = 1024
+TILE = 2048
 FORWARD = 1024
 ROWS = 512
 
@@ -194,7 +194,7 @@
         down_rows = pl.ds(pl.multiple_of(k * WIDE, WIDE), width)
 
         def hidden(t, carry):
-            rows = at(t, 2 * TILE)
+            rows = at(t, TILE)
             gu = dot(a_ref[rows, :], wgu_ref[layer, :, gu_cols])
             dh = dot_t(g_ref[rows, :], wd_ref[layer, down_rows, :]).astype(BF16).astype(F32)
             gate, up = gu[:, :width], gu[:, width:]
@@ -205,7 +205,7 @@
             dgu_ref[rows, pl.ds(0, width)] = (dh * up * (s + silu * (1.0 - s))).astype(BF16)
             return carry
 
-        lax.fori_loop(0, tokens // (2 * TILE), hidden, 0)
+        lax.fori_loop(0, tokens // TILE, hidden, 0)
         if layer:
             when(k == 0, start_two, layer, last)
             when((k >= 1) & (k < full), start_two, layer, k - 1)
@@ -341,16 +341,23 @@
 
         @pl.when((pl.program_id(0) >= start) & (pl.program_id(0) < start + steps))
         def _(mine=mine):
-            for j in range(units // LANES):
-                cols = pl.ds(j * LANES, LANES)
+            def unit(j, carry, mine=mine):
+                cols = at(j, LANES)
                 for i in range(3):
-                    g = [ref[:, pl.ds((3 * j + i) * LANES, LANES)].astype(F32) for ref in mine]
+                    g = [ref[:, at(3 * j + i, LANES)].astype(F32) for ref in mine]
                     g = jnp.concatenate(g, 0) if len(g) > 1 else g[0]
                     index = (0, slice(None), cols)
                     if i == 2:
                         g, index = g.T, (0, cols, slice(None))
                     w, m, v = adamw(ins[i][index].astype(F32), ins[3 + i][index], ins[6 + i][index], g)
                     outs[i][index], outs[3 + i][index], outs[6 + i][index] = w, m, v
+                return carry
+
+            if len(sources) == 1:
+                for j in range(units // LANES):
+                    unit(j, 0)
+            else:
+                lax.fori_loop(0, units // LANES, unit, 0)
 
         start += steps
 

time: 239 us -> 237 us (level)
  no operation moved by 1% of the time
where the time goes in v5:
time: 237 us
  Pallas kernels  226 us (95%)
  starting transfers between devices  5.9 us (2%)
  waiting for transfers between devices  3.01 us (1%)
    pallas_call x1, Pallas kernels, main_call(): pl.pallas_call(functools.partial(main_kernel, n), out_shape=[jax.ShapeDty...  181 us
    pallas_call x3, Pallas kernels, adam_call(): pl.pallas_call(functools.partial(adam_kernel, steps), grid_spec=pltpu.Pre...  45.4 us
  transfers between devices with their start and end apart: 4, of which 2 were waited for; matrix products, arithmetic and copies ran while one was open for 0% of the time, Pallas kernels for 16%

profile of v5, /device:TPU:112, one launch (start us, length us, event | category | flops | bytes accessed | tf_op | source)
XLA Modules:
  0.0 237.4 jit_solution(16910987242500834422)
XLA Ops:
  0.6 181.0 %main.1 = (bf16[512,4992]{1,0:T(8,128)(2,1)}, bf16[128,4992]{1,0:T(8,128)(2,1)}) custom-call(bf16[1,4096,512]{2,1,0:T(8,128)(2,1)} %x_hbm, bf16[1,4096,512]{2,1,0:T(8,128)(2,1)} %dy_hbm.1, bf16[2,512,1664]{2,1,0:T(8,128)(2,1)} %refs_2_.5, bf16[2,512,1664]{2,1,0:T(8,128)(2,1)} %refs_3_.5, bf16[2,1664,512]{2,1,0:T(8,128)(2,1)} %refs_4_.5), custom_call_target="tpu_custom_call" | custom-call | tf_op jit(solution)/shard_map/main/pallas_call | solution.py:296
  181.7 2.6 %collective-permute-start.1 = (bf16[128,4992]{1,0:T(8,128)(2,1)}, bf16[128,4992]{1,0:T(8,128)(2,1)S(1)}, u32[]{:S(2)}, u32[]{:S(2)}) collective-permute-start(bf16[128,4992]{1,0:T(8,128)(2,1)} %get-tuple-element.44.refs_1_), channel_id=1, source_target_pairs={{0,3},{1,0},{2,1},{3,2},{4,7},{5,4},{6,5},{7,6},{8,11},{9,8},{10,9... | collective-permute-start | bytes 3833864 | tf_op jit(solution)/shard_map/ppermute | solution.py:422
  184.3 0.0 collective-permute-start
  184.3 27.9 %adam.3 = (bf16[2,512,1664]{2,1,0:T(8,128)(2,1)}, bf16[2,512,1664]{2,1,0:T(8,128)(2,1)}, bf16[2,1664,512]{2,1,0:T(8,128)(2,1)}, f32[2,512,1664]{2,1,0:T(8,128)},...) custom-call(s32[1]{0:T(128)} %bitcast.me, ...), custom_call_target="tpu_custom_call" | custom-call | flops 1916928000 | bytes 70287360 | tf_op jit(solution)/shard_map/adam/pallas_call | solution.py:389
  212.2 0.0 collective-permute-done.1.refs_1_
  212.2 0.0 copy-start
  212.2 1.9 collective-permute-done.refs_0_
  214.1 0.0 copy-start.1
  214.2 0.1 collective-permute-start.2
  214.3 3.2 %collective-permute-start.3 = (bf16[64,4992]{1,0:T(8,128)(2,1)S(1)}, bf16[64,4992]{1,0:T(8,128)(2,1)S(1)}, u32[]{:S(2)}, u32[]{:S(2)}) collective-permute-start(bf16[64,4992]{1,0:T(8,128)(2,1)S(1)} %slice.7), channel_id=1, source_target_pairs={{0,3},{1,0},{2,1},{3,2},{4,7},{5,4},{6,5},{7,6},{8,11},{9,8},{10,9... | collective-permute-start | bytes 1916936 | tf_op jit(solution)/shard_map/ppermute | solution.py:425
  217.5 0.0 copy-done
  217.5 0.0 copy-done.1
  217.5 10.9 %adam.4 = (bf16[2,512,1664]{2,1,0:T(8,128)(2,1)}, bf16[2,512,1664]{2,1,0:T(8,128)(2,1)}, bf16[2,1664,512]{2,1,0:T(8,128)(2,1)}, f32[2,512,1664]{2,1,0:T(8,128)},...) custom-call(s32[1]{0:T(128)} %bitcast.me, ...), custom_call_target="tpu_custom_call", output_to_operand_aliasing={{0}: (12, {}), {1}: (13, {}), {2}: (14, {}), {3}: (15, {}),... | custom-call | flops 766771200 | bytes 28114944 | tf_op jit(solution)/shard_map/adam/pallas_call | solution.py:389
  228.5 1.1 collective-permute-done.2.refs_0_
  229.6 0.0 copy-start.2
  229.6 0.0 collective-permute-done.3.refs_1_
  229.6 0.0 copy-start.3
  229.6 0.8 copy-done.2
  230.4 0.2 copy-done.3
  230.6 6.6 %adam.5 = (bf16[2,512,1664]{2,1,0:T(8,128)(2,1)}, bf16[2,512,1664]{2,1,0:T(8,128)(2,1)}, bf16[2,1664,512]{2,1,0:T(8,128)(2,1)}, f32[2,512,1664]{2,1,0:T(8,128)},...) custom-call(s32[1]{0:T(128)} %bitcast.me, ...), custom_call_target="tpu_custom_call", output_to_operand_aliasing={{0}: (12, {}), {1}: (13, {}), {2}: (14, {}), {3}: (15, {}),... | custom-call | flops 383385600 | bytes 14057472 | tf_op jit(solution)/shard_map/adam/pallas_call | solution.py:389
  (2 shorter events, 0.1 us)
Async XLA Ops:
  181.7 30.5 %collective-permute-start.1 = (bf16[128,4992]{1,0:T(8,128)(2,1)}, bf16[128,4992]{1,0:T(8,128)(2,1)S(1)}, u32[]{:S(2)}, u32[]{:S(2)}) collective-permute-start(bf16[128,4992]{1,0:T(8,128)(2,1)} %get-tuple-element.44.refs_1_), channel_id=1, source_target_pairs={{0,3},{1,0},{2,1},{3,2},{4,7},{5,4},{6,5},{7,6},{8,11},{9,8},{10,9... | collective-permute-start | bytes 3833864 | tf_op jit(solution)/shard_map/ppermute | solution.py:422
  184.3 29.8 %collective-permute-start = (bf16[128,4992]{1,0:T(8,128)(2,1)}, bf16[128,4992]{1,0:T(8,128)(2,1)S(1)}, u32[]{:S(2)}, u32[]{:S(2)}) collective-permute-start(bf16[128,4992]{1,0:T(8,128)(2,1)} %get-tuple-element.44.refs_1_), channel_id=1, source_target_pairs={{0,1},{1,2},{2,3},{3,0},{4,5},{5,6},{6,7},{7,4},{8,9},{9,10},{10,1... | collective-permute-start | bytes 3833864 | tf_op jit(solution)/shard_map/ppermute | solution.py:422
  212.2 5.3 %copy-start = (bf16[128,4992]{1,0:T(8,128)(2,1)}, bf16[128,4992]{1,0:T(8,128)(2,1)S(1)}, u32[]{:S(2)}) copy-start(bf16[128,4992]{1,0:T(8,128)(2,1)S(1)} %collective-permute-done.1.refs_1_) | copy-start | bytes 3833860
  214.1 3.4 %copy-start.1 = (bf16[128,4992]{1,0:T(8,128)(2,1)}, bf16[128,4992]{1,0:T(8,128)(2,1)S(1)}, u32[]{:S(2)}) copy-start(bf16[128,4992]{1,0:T(8,128)(2,1)S(1)} %collective-permute-done.refs_0_) | copy-start | bytes 3833860
  214.2 15.4 %collective-permute-start.2 = (bf16[64,4992]{1,0:T(8,128)(2,1)S(1)}, bf16[64,4992]{1,0:T(8,128)(2,1)S(1)}, u32[]{:S(2)}, u32[]{:S(2)}) collective-permute-start(bf16[64,4992]{1,0:T(8,128)(2,1)S(1)} %slice.6), channel_id=1, source_target_pairs={{0,1},{1,2},{2,3},{3,0},{4,5},{5,6},{6,7},{7,4},{8,9},{9,10},{10,1... | collective-permute-start | bytes 1916936 | tf_op jit(solution)/shard_map/ppermute | solution.py:425
  214.3 15.3 %collective-permute-start.3 = (bf16[64,4992]{1,0:T(8,128)(2,1)S(1)}, bf16[64,4992]{1,0:T(8,128)(2,1)S(1)}, u32[]{:S(2)}, u32[]{:S(2)}) collective-permute-start(bf16[64,4992]{1,0:T(8,128)(2,1)S(1)} %slice.7), channel_id=1, source_target_pairs={{0,3},{1,0},{2,1},{3,2},{4,7},{5,4},{6,5},{7,6},{8,11},{9,8},{10,9... | collective-permute-start | bytes 1916936 | tf_op jit(solution)/shard_map/ppermute | solution.py:425
  229.6 0.8 copy-start.2
  229.6 1.1 copy-start.3

commit v6 on v5

--- a/solution.py
+++ b/solution.py
@@ -217,7 +217,7 @@
 
         else:
             when(k >= 3, finish, layer, k - 3)
-            when(k + 3 < full, start_far, k + 3)
+            when(k + 4 < full, start_far, k + 4)
         dgu = dot(at_ref[...], dgu_ref[:, pl.ds(0, 2 * width)]).astype(BF16)
         down = dot(gt_ref[...], hid_ref[:, pl.ds(0, width)]).astype(BF16)
         for j in range(width // LANES):
@@ -239,7 +239,10 @@
 
             lax.fori_loop(0, tokens // TILE, by_a, 0)
             when(k == 0, finish, layer, last)
-            when((k >= 2) & (k < full), finish, layer, k - 2)
+            when(k == 1, finish, layer, 0)
+            when(k == 2, start_far, last)
+            when(k == 2, start_far, 0)
+            when((k >= 3) & (k < full), finish, layer, k - 2)
 
     last = len(widths) - 1
     pl.semaphore_wait(barrier, 2)
@@ -266,12 +269,11 @@
     lax.fori_loop(0, steps // 4, between, 0)
     start_two(1, full - 1)
     finish(1, full - 2)
-    start_far(last)
-    start_far(0)
+    start_far(1)
+    start_far(2)
     lax.fori_loop(steps // 4, steps, between, 0)
     finish(1, full - 1)
-    start_far(1)
-    start_far(2)
+    start_far(3)
     lax.fori_loop(0, full, lambda k, carry: (chunk(0, k, WIDE, False), carry)[1], 0)
     chunk(0, last, widths[last], False)
     finish(0, last - 2)

time: 237 us -> 236 us (level)
  no operation moved by 1% of the time
where the time goes in v6:
time: 236 us
  Pallas kernels  226 us (96%)
  starting transfers between devices  5.45 us (2%)
  waiting for transfers between devices  3.01 us (1%)
    pallas_call x1, Pallas kernels, main_call(): pl.pallas_call(functools.partial(main_kernel, n), out_shape=[jax.ShapeDty...  180 us
    pallas_call x3, Pallas kernels, adam_call(): pl.pallas_call(functools.partial(adam_kernel, steps), grid_spec=pltpu.Pre...  45.4 us
  transfers between devices with their start and end apart: 4, of which 2 were waited for; matrix products, arithmetic and copies ran while one was open for 0% of the time, Pallas kernels for 16%

profile of v6, /device:TPU:112, one launch (start us, length us, event | category | flops | bytes accessed | tf_op | source)
XLA Modules:
  0.0 236.1 jit_solution(16656521279045813001)
XLA Ops:
  0.6 180.2 %main.1 = (bf16[512,4992]{1,0:T(8,128)(2,1)}, bf16[128,4992]{1,0:T(8,128)(2,1)}) custom-call(bf16[1,4096,512]{2,1,0:T(8,128)(2,1)} %x_hbm, bf16[1,4096,512]{2,1,0:T(8,128)(2,1)} %dy_hbm.1, bf16[2,512,1664]{2,1,0:T(8,128)(2,1)} %refs_2_.5, bf16[2,512,1664]{2,1,0:T(8,128)(2,1)} %refs_3_.5, bf16[2,1664,512]{2,1,0:T(8,128)(2,1)} %refs_4_.5), custom_call_target="tpu_custom_call" | custom-call | tf_op jit(solution)/shard_map/main/pallas_call | solution.py:298
  180.8 2.1 collective-permute-start.1
  183.0 0.0 collective-permute-start
  183.0 27.9 %adam.3 = (bf16[2,512,1664]{2,1,0:T(8,128)(2,1)}, bf16[2,512,1664]{2,1,0:T(8,128)(2,1)}, bf16[2,1664,512]{2,1,0:T(8,128)(2,1)}, f32[2,512,1664]{2,1,0:T(8,128)},...) custom-call(s32[1]{0:T(128)} %bitcast.me, ...), custom_call_target="tpu_custom_call" | custom-call | flops 1916928000 | bytes 70287360 | tf_op jit(solution)/shard_map/adam/pallas_call | solution.py:391
  210.9 0.0 collective-permute-done.1.refs_1_
  210.9 0.0 copy-start
  210.9 1.9 collective-permute-done.refs_0_
  212.8 0.0 copy-start.1
  212.9 0.1 collective-permute-start.2
  213.0 3.2 %collective-permute-start.3 = (bf16[64,4992]{1,0:T(8,128)(2,1)S(1)}, bf16[64,4992]{1,0:T(8,128)(2,1)S(1)}, u32[]{:S(2)}, u32[]{:S(2)}) collective-permute-start(bf16[64,4992]{1,0:T(8,128)(2,1)S(1)} %slice.7), channel_id=1, source_target_pairs={{0,3},{1,0},{2,1},{3,2},{4,7},{5,4},{6,5},{7,6},{8,11},{9,8},{10,9... | collective-permute-start | bytes 1916936 | tf_op jit(solution)/shard_map/ppermute | solution.py:427
  216.2 0.0 copy-done
  216.2 0.0 copy-done.1
  216.2 10.9 %adam.4 = (bf16[2,512,1664]{2,1,0:T(8,128)(2,1)}, bf16[2,512,1664]{2,1,0:T(8,128)(2,1)}, bf16[2,1664,512]{2,1,0:T(8,128)(2,1)}, f32[2,512,1664]{2,1,0:T(8,128)},...) custom-call(s32[1]{0:T(128)} %bitcast.me, ...), custom_call_target="tpu_custom_call", output_to_operand_aliasing={{0}: (12, {}), {1}: (13, {}), {2}: (14, {}), {3}: (15, {}),... | custom-call | flops 766771200 | bytes 28114944 | tf_op jit(solution)/shard_map/adam/pallas_call | solution.py:391
  227.1 1.1 collective-permute-done.2.refs_0_
  228.2 0.0 copy-start.2
  228.3 0.0 collective-permute-done.3.refs_1_
  228.3 0.0 copy-start.3
  228.3 0.8 copy-done.2
  229.1 0.2 copy-done.3
  229.3 6.6 %adam.5 = (bf16[2,512,1664]{2,1,0:T(8,128)(2,1)}, bf16[2,512,1664]{2,1,0:T(8,128)(2,1)}, bf16[2,1664,512]{2,1,0:T(8,128)(2,1)}, f32[2,512,1664]{2,1,0:T(8,128)},...) custom-call(s32[1]{0:T(128)} %bitcast.me, ...), custom_call_target="tpu_custom_call", output_to_operand_aliasing={{0}: (12, {}), {1}: (13, {}), {2}: (14, {}), {3}: (15, {}),... | custom-call | flops 383385600 | bytes 14057472 | tf_op jit(solution)/shard_map/adam/pallas_call | solution.py:391
  (2 shorter events, 0.1 us)
Async XLA Ops:
  180.8 30.0 %collective-permute-start.1 = (bf16[128,4992]{1,0:T(8,128)(2,1)}, bf16[128,4992]{1,0:T(8,128)(2,1)S(1)}, u32[]{:S(2)}, u32[]{:S(2)}) collective-permute-start(bf16[128,4992]{1,0:T(8,128)(2,1)} %get-tuple-element.44.refs_1_), channel_id=1, source_target_pairs={{0,3},{1,0},{2,1},{3,2},{4,7},{5,4},{6,5},{7,6},{8,11},{9,8},{10,9... | collective-permute-start | bytes 3833864 | tf_op jit(solution)/shard_map/ppermute | solution.py:424
  183.0 29.8 %collective-permute-start = (bf16[128,4992]{1,0:T(8,128)(2,1)}, bf16[128,4992]{1,0:T(8,128)(2,1)S(1)}, u32[]{:S(2)}, u32[]{:S(2)}) collective-permute-start(bf16[128,4992]{1,0:T(8,128)(2,1)} %get-tuple-element.44.refs_1_), channel_id=1, source_target_pairs={{0,1},{1,2},{2,3},{3,0},{4,5},{5,6},{6,7},{7,4},{8,9},{9,10},{10,1... | collective-permute-start | bytes 3833864 | tf_op jit(solution)/shard_map/ppermute | solution.py:424
  210.9 5.3 %copy-start = (bf16[128,4992]{1,0:T(8,128)(2,1)}, bf16[128,4992]{1,0:T(8,128)(2,1)S(1)}, u32[]{:S(2)}) copy-start(bf16[128,4992]{1,0:T(8,128)(2,1)S(1)} %collective-permute-done.1.refs_1_) | copy-start | bytes 3833860
  212.8 3.4 %copy-start.1 = (bf16[128,4992]{1,0:T(8,128)(2,1)}, bf16[128,4992]{1,0:T(8,128)(2,1)S(1)}, u32[]{:S(2)}) copy-start(bf16[128,4992]{1,0:T(8,128)(2,1)S(1)} %collective-permute-done.refs_0_) | copy-start | bytes 3833860
  212.9 15.4 %collective-permute-start.2 = (bf16[64,4992]{1,0:T(8,128)(2,1)S(1)}, bf16[64,4992]{1,0:T(8,128)(2,1)S(1)}, u32[]{:S(2)}, u32[]{:S(2)}) collective-permute-start(bf16[64,4992]{1,0:T(8,128)(2,1)S(1)} %slice.6), channel_id=1, source_target_pairs={{0,1},{1,2},{2,3},{3,0},{4,5},{5,6},{6,7},{7,4},{8,9},{9,10},{10,1... | collective-permute-start | bytes 1916936 | tf_op jit(solution)/shard_map/ppermute | solution.py:427
  213.0 15.3 %collective-permute-start.3 = (bf16[64,4992]{1,0:T(8,128)(2,1)S(1)}, bf16[64,4992]{1,0:T(8,128)(2,1)S(1)}, u32[]{:S(2)}, u32[]{:S(2)}) collective-permute-start(bf16[64,4992]{1,0:T(8,128)(2,1)S(1)} %slice.7), channel_id=1, source_target_pairs={{0,3},{1,0},{2,1},{3,2},{4,7},{5,4},{6,5},{7,6},{8,11},{9,8},{10,9... | collective-permute-start | bytes 1916936 | tf_op jit(solution)/shard_map/ppermute | solution.py:427
  228.2 0.8 copy-start.2
  228.3 1.1 copy-start.3
